TPU v7x, 16 devices: a whole 2x2x2 slice. The times are simulated.
16 devices in a mesh: data: 16 (over z, y, x, core).
Axes of the slice: x: 2, y: 2, z: 2, core: 2. Of those that a mesh axis runs over, the one named last changes fastest.
Arguments:
- x_in: bfloat16 [48, 512, 2048], P('data')
- dy_out: bfloat16 [48, 512, 2048], P('data')
- lengths: int32 [48], P('data')
- w_up: bfloat16 [2, 2048, 8192], replicated
- w_down: bfloat16 [2, 8192, 2048], replicated
- noise_up: float32 [2, 2048, 8192], replicated
- noise_down: float32 [2, 8192, 2048], replicated
- clip_norm: float32 [2], replicated
Outputs:
- output 1: float32 [2, 2048, 8192], replicated
- output 2: float32 [2, 8192, 2048], replicated
All inputs are finite; a program needn't handle non-finite values.
Results may differ from a plain program's by a relative error of at most 0.0112315.
Values are sent between devices in bfloat16 or wider.
A program may use at most 2.75 GiB of HBM per device.

v0:
```python
import functools
import jax
import jax.numpy as jnp
from jax import lax
from jax.sharding import PartitionSpec as P


def gelu_grad(hidden):
    return 0.5 * (1.0 + lax.erf(hidden * 0.7071067811865476)) + hidden * jnp.exp(-0.5 * hidden * hidden) * 0.3989422804014327


def gram_of(matrix):
    return jnp.einsum('btk,bsk->bts', matrix, matrix, preferred_element_type=jnp.float32)


def per_device(x_in, dy_out, lengths, w_up, w_down, noise_up, noise_down, clip_norm, batch_total):
    n_layers = w_up.shape[0]
    seq_len = x_in.shape[1]
    tok_mask = (jnp.arange(seq_len)[None, :] < lengths[:, None]).astype(jnp.bfloat16)
    grad_cur = dy_out * tok_mask[:, :, None]
    x_cur = x_in
    saved = []
    for layer_idx in range(n_layers):
        hidden = jnp.einsum('btd,df->btf', x_cur, w_up[layer_idx], preferred_element_type=jnp.float32).astype(jnp.bfloat16)
        gelu_out = jax.nn.gelu(hidden.astype(jnp.float32), approximate=False).astype(jnp.bfloat16)
        saved.append((x_cur, hidden, gelu_out))
        if layer_idx < n_layers - 1:
            block_out = jnp.einsum('btf,fd->btd', gelu_out, w_down[layer_idx], preferred_element_type=jnp.float32)
            x_cur = (x_cur.astype(jnp.float32) + block_out).astype(jnp.bfloat16)
    up_grads = [None] * n_layers
    down_grads = [None] * n_layers
    for layer_idx in reversed(range(n_layers)):
        x_cur, hidden, gelu_out = saved[layer_idx]
        grad_act = jnp.einsum('btd,fd->btf', grad_cur, w_down[layer_idx], preferred_element_type=jnp.float32)
        grad_pre = (grad_act * gelu_grad(hidden.astype(jnp.float32))).astype(jnp.bfloat16)
        norm_sq = jnp.sum(gram_of(gelu_out) * gram_of(grad_cur) + gram_of(x_cur) * gram_of(grad_pre), axis=(1, 2))
        factor = jnp.minimum(1.0, clip_norm[layer_idx] / jnp.sqrt(norm_sq))[:, None, None]
        up_part = jnp.einsum('btd,btf->df', x_cur, (grad_pre * factor).astype(jnp.bfloat16), preferred_element_type=jnp.float32)
        down_part = jnp.einsum('btf,btd->fd', gelu_out, (grad_cur * factor).astype(jnp.bfloat16), preferred_element_type=jnp.float32)
        up_red, down_red = lax.psum((up_part.astype(jnp.bfloat16), down_part.astype(jnp.bfloat16)), 'data')
        up_grads[layer_idx] = (up_red.astype(jnp.float32) + noise_up[layer_idx]) / batch_total
        down_grads[layer_idx] = (down_red.astype(jnp.float32) + noise_down[layer_idx]) / batch_total
        if layer_idx > 0:
            back_term = jnp.einsum('btf,df->btd', grad_pre, w_up[layer_idx], preferred_element_type=jnp.float32)
            grad_cur = (grad_cur.astype(jnp.float32) + back_term).astype(jnp.bfloat16)
    return jnp.stack(up_grads), jnp.stack(down_grads)


def solution(mesh):
    batch_spec = P('data', None, None)

    def grad_step(x_in, dy_out, lengths, w_up, w_down, noise_up, noise_down, clip_norm):
        device_fn = functools.partial(per_device, batch_total=x_in.shape[0])
        mapped = jax.shard_map(device_fn, mesh=mesh, in_specs=(batch_spec, batch_spec, P('data'), P(), P(), P(), P(), P()), out_specs=(P(), P()), check_vma=False)
        return mapped(x_in, dy_out, lengths, w_up, w_down, noise_up, noise_down, clip_norm)

    return grad_step
```

profile of v0, /device:TPU:0, one launch (start us, length us, event | category | flops | bytes accessed | tf_op | source)
XLA Modules:
  0.0 2371.3 jit_solution(16670785776074332672)
XLA Ops:
  7.2 0.0 all-reduce.6.cloned.1.call-start
  7.2 0.7 fusion.135
  7.9 9.9 fusion.129
  17.8 5.9 fusion.189
  23.7 0.0 copy-done.2
  23.7 9.7 fusion.140
  33.4 66.6 %fusion.119 = (u8[512,8192]{1,0:T(8,128)(4,1)S(1)}, bf16[3,512,8192]{2,1,0:T(8,128)(2,1)}) fusion(bf16[3,512,2048]{2,1,0:T(8,128)(2,1)} %param.8, bf16[2,2048,8192]{2,1,0:T(8,128)(2,1)} %param.11), kind=kOutput, calls=%fused_computation.146 | convolution fusion | flops 51648659456 | bytes 69206016 | tf_op jit(solution)/shard_map/btd,df->btf/dot_general | solution.py:24
  100.0 113.9 %fusion.10 = bf16[3,512,8192]{2,1,0:T(8,128)(2,1)} fusion(bf16[3,512,8192]{2,1,0:T(8,128)(2,1)} %get-tuple-element.14, u8[512,8192]{1,0:T(8,128)(4,1)S(1)} %get-tuple-element.13), kind=kLoop, calls=%fused_computation.34 | loop fusion | flops 868220928 | bytes 54525952 | tf_op jit(solution)/shard_map/convert_element_type | solution.py:25
  213.9 22.9 fusion.138
  236.8 66.7 %add_convert_fusion = bf16[3,512,2048]{2,1,0:T(8,128)(2,1)S(1)} fusion(bf16[3,512,2048]{2,1,0:T(8,128)(2,1)} %param.8, bf16[3,512,8192]{2,1,0:T(8,128)(2,1)} %fusion.10, bf16[2,8192,2048]{2,1,0:T(8,128)(2,1)} %param.12), kind=kOutput, calls=%fused_computation.145 | convolution fusion | flops 51549044736 | bytes 71303168 | tf_op jit(solution)/shard_map/btf,fd->btd/dot_general | solution.py:28
  303.5 0.0 copy-start.7
  303.5 2.6 copy-done.7
  306.1 5.1 fusion.142
  311.2 68.4 %fusion.120 = (u8[512,8192]{1,0:T(8,128)(4,1)}, bf16[3,512,8192]{2,1,0:T(8,128)(2,1)}) fusion(bf16[3,512,2048]{2,1,0:T(8,128)(2,1)} %copy-done.7, bf16[2,2048,8192]{2,1,0:T(8,128)(2,1)} %param.11), kind=kOutput, calls=%fused_computation.147 | convolution fusion | flops 51648659456 | bytes 69206016 | tf_op jit(solution)/shard_map/btd,df->btf/dot_general | solution.py:24
  379.6 77.7 %fusion.84 = bf16[3,512,8192]{2,1,0:T(8,128)(2,1)} fusion(bf16[3,512,8192]{2,1,0:T(8,128)(2,1)} %get-tuple-element.16, bf16[2,8192,2048]{2,1,0:T(8,128)(2,1)} %param.12, bf16[3,512,2048]{2,1,0:T(8,128)(2,1)} %fusion.189), kind=kOutput, calls=%fused_computation.115 | convolution fusion | flops 51678019584 | bytes 90177536 | tf_op jit(solution)/shard_map/btd,fd->btf/dot_general | solution.py:34
  457.3 0.0 copy-done.3
  457.3 68.0 %fusion.117 = bf16[3,512,2048]{2,1,0:T(8,128)(2,1)} fusion(bf16[3,512,8192]{2,1,0:T(8,128)(2,1)} %fusion.84, bf16[2,2048,8192]{2,1,0:T(8,128)(2,1)} %param.11, bf16[3,512,2048]{2,1,0:T(8,128)(2,1)} %param.9, bf16[3,512]{1,0:T(4,128)(2,1)S(1)} %copy-done.3), kind=kOutput, calls=%fused_computation.142 | convolution fusion | flops 51552190464 | bytes 71306240 | tf_op jit(solution)/shard_map/btf,df->btd/dot_general | solution.py:44
  525.3 79.3 %fusion.85 = bf16[3,512,8192]{2,1,0:T(8,128)(2,1)} fusion(bf16[3,512,8192]{2,1,0:T(8,128)(2,1)} %get-tuple-element.14, bf16[3,512,2048]{2,1,0:T(8,128)(2,1)} %fusion.117, bf16[2,8192,2048]{2,1,0:T(8,128)(2,1)} %param.12), kind=kOutput, calls=%fused_computation.116 | convolution fusion | flops 51678019584 | bytes 90177536 | tf_op jit(solution)/shard_map/btd,fd->btf/dot_general | solution.py:34
  604.5 0.0 copy-done.6
  604.6 5.1 fusion.139
  609.7 0.0 copy-done.5
  609.7 0.6 fusion.137
  610.3 0.0 copy-done.1
  610.3 114.1 %fusion.13 = bf16[3,512,8192]{2,1,0:T(8,128)(2,1)} fusion(bf16[3,512,8192]{2,1,0:T(8,128)(2,1)} %get-tuple-element.16, u8[512,8192]{1,0:T(8,128)(4,1)S(1)} %copy-done.1), kind=kLoop, calls=%fused_computation.37 | loop fusion | flops 868220928 | bytes 54525952 | tf_op jit(solution)/shard_map/convert_element_type | solution.py:25
  724.5 22.7 fusion.141
  747.1 0.0 copy-done.9
  747.1 26.1 %add_reduce_fusion = f32[3]{0:T(128)S(1)} fusion(f32[3,512,512]{2,1,0:T(8,128)S(1)} %copy-done.9, f32[3,512,512]{2,1,0:T(8,128)} %fusion.141, f32[3,512,512]{2,1,0:T(8,128)} %fusion.129, bf16[3,512,8192]{2,1,0:T(8,128)(2,1)} %fusion.84), kind=kOutput, calls=%fused_computation.154 | convolution fusion | flops 12888047616 | bytes 34603020 | tf_op jit(solution)/shard_map/btk,bsk->bts/dot_general | solution.py:13
  773.2 0.7 multiply_minimum_fusion
  773.9 0.0 copy-start
  773.9 62.6 %bitcast_convert_fusion.2 = bf16[2048,8192]{0,1:T(8,128)(2,1)} fusion(bf16[3,512,2048]{2,1,0:T(8,128)(2,1)} %copy-done.7, bf16[3,512,8192]{2,1,0:T(8,128)(2,1)} %fusion.84, f32[3]{0:T(128)S(1)} %multiply_minimum_fusion), kind=kOutput, calls=%fused_computation.27 | convolution fusion | flops 51594133504 | bytes 65011724 | tf_op jit(solution)/shard_map/btd,btf->df/dot_general | solution.py:38
  836.6 64.9 %bitcast_convert_fusion = bf16[8192,2048]{1,0:T(8,128)(2,1)} fusion(bf16[3,512,8192]{2,1,0:T(8,128)(2,1)} %fusion.13, f32[3]{0:T(128)S(1)} %multiply_minimum_fusion, bf16[3,512,2048]{2,1,0:T(8,128)(2,1)S(1)} %copy-done, bf16[3,512]{1,0:T(4,128)(2,1)S(1)} %copy-done.4), kind=kOutput, calls=%fused_computation.19 | convolution fusion | flops 51568967680 | bytes 65014796 | tf_op jit(solution)/shard_map/btf,btd->fd/dot_general | solution.py:39
  901.5 25.9 %add_reduce_fusion.1 = f32[3]{0:T(128)S(1)} fusion(f32[3,512,512]{2,1,0:T(8,128)S(1)} %copy-done.8, f32[3,512,512]{2,1,0:T(8,128)} %fusion.138, f32[3,512,512]{2,1,0:T(8,128)} %fusion.139, bf16[3,512,8192]{2,1,0:T(8,128)(2,1)} %fusion.85), kind=kOutput, calls=%fused_computation.155 | convolution fusion | flops 12888047616 | bytes 34603020 | tf_op jit(solution)/shard_map/btk,bsk->bts/dot_general | solution.py:13
  927.4 0.6 multiply_minimum_fusion.1
  927.9 61.8 %fusion.104 = bf16[2048,8192]{0,1:T(8,128)(2,1)} fusion(bf16[3,512,2048]{2,1,0:T(8,128)(2,1)} %param.8, bf16[3,512,8192]{2,1,0:T(8,128)(2,1)} %fusion.85, f32[3]{0:T(128)S(1)} %multiply_minimum_fusion.1), kind=kOutput, calls=%fused_computation.135 | convolution fusion | flops 51594133504 | bytes 65011724 | tf_op jit(solution)/shard_map/btd,btf->df/dot_general | solution.py:38
  989.7 0.0 all-reduce.6.cloned.1.call-update
  989.8 0.0 all-reduce.4.cloned.1.call-start
  989.8 63.6 %bitcast_convert_fusion.1 = bf16[8192,2048]{1,0:T(8,128)(2,1)} fusion(bf16[3,512,8192]{2,1,0:T(8,128)(2,1)} %fusion.10, bf16[3,512,2048]{2,1,0:T(8,128)(2,1)} %fusion.117, f32[3]{0:T(128)S(1)} %multiply_minimum_fusion.1), kind=kOutput, calls=%fused_computation.23 | convolution fusion | flops 51565821952 | bytes 65011724 | tf_op jit(solution)/shard_map/btf,btd->fd/dot_general | solution.py:39
  1053.4 0.0 all-reduce.4.cloned.1.call-update
  1053.4 84.5 %fusion.136 = (f32[1,2048,8192]{2,1,0:T(8,128)}, f32[1,2048,8192]{2,1,0:T(8,128)}) fusion(f32[2,2048,8192]{2,1,0:T(8,128)} %param.13), kind=kLoop, calls=%fused_computation.163 | loop fusion | bytes 268435456 | tf_op jit(solution)/shard_map/slice | solution.py:41
  1137.9 66.1 %copy.24 = f32[1,2048,8192]{1,2,0:T(8,128)} copy(f32[1,2048,8192]{2,1,0:T(8,128)} %get-tuple-element.9) | data formatting | bytes 134217728
  1204.0 66.0 %copy.25 = f32[1,2048,8192]{1,2,0:T(8,128)} copy(f32[1,2048,8192]{2,1,0:T(8,128)} %get-tuple-element.10) | data formatting | bytes 134217728
  1270.0 580.9 %all-reduce.6.cloned.1.call-done = (bf16[2048,8192]{0,1:T(8,128)(2,1)}, bf16[2048,8192]{0,1:T(8,128)(2,1)}, bf16[8192,2048]{1,0:T(8,128)(2,1)}) async-done(((bf16[2048,8192]{0,1:T(8,128)(2,1)}, bf16[2048,8192]{0,1:T(8,128)(2,1)}, bf16[8192,2048]{1,0:T(8,128)(2,1)}), (bf16[2048,8192]{0,1:T(8,128)(2,1)}, bf16[2048,8192]{0,1:T(8,128)(2,1)}, bf16[8192,2048]{1,0:T(8,128)(2,1)})) %all-reduce.6.cloned.1.call-update) | async-done | bytes 100663312 | tf_op jit(solution)/shard_map/psum | solution.py:40
  1850.9 105.2 %fusion.5 = (f32[1,2048,8192]{1,2,0:T(8,128)}, f32[1,2048,8192]{1,2,0:T(8,128)}) fusion(f32[1,2048,8192]{1,2,0:T(8,128)} %copy.25, bf16[2048,8192]{0,1:T(8,128)(2,1)} %get-tuple-element.4, f32[1,2048,8192]{1,2,0:T(8,128)} %copy.24, bf16[2048,8192]{0,1:T(8,128)(2,1)} %get-tuple-element.5), kind=kLoop, calls=%fused_computation.26 | loop fusion | flops 100663296 | bytes 335544320 | tf_op jit(solution)/shard_map/stack | solution.py:46
  1956.1 85.5 %pad_maximum_fusion = f32[2,2048,8192]{1,2,0:T(8,128)} fusion(f32[1,2048,8192]{1,2,0:T(8,128)} %get-tuple-element.17, f32[1,2048,8192]{1,2,0:T(8,128)} %get-tuple-element.18), kind=kLoop, calls=%fused_computation | loop fusion | flops 33554432 | bytes 268435456 | tf_op jit(solution)/shard_map/stack | solution.py:46
  2041.6 121.5 %copy.17 = f32[2,2048,8192]{2,1,0:T(8,128)} copy(f32[2,2048,8192]{1,2,0:T(8,128)} %pad_maximum_fusion) | data formatting | bytes 268435456
  2163.1 10.3 all-reduce.4.cloned.1.call-done
  2173.4 105.1 %fusion.3 = (f32[1,8192,2048]{2,1,0:T(8,128)}, f32[1,8192,2048]{2,1,0:T(8,128)}) fusion(f32[2,8192,2048]{2,1,0:T(8,128)} %param.14, bf16[8192,2048]{1,0:T(8,128)(2,1)} %all-reduce.4.cloned.1.call-done, bf16[8192,2048]{1,0:T(8,128)(2,1)} %get-tuple-element.6), kind=kLoop, calls=%fused_computation.22 | loop fusion | flops 100663296 | bytes 335544320 | tf_op jit(solution)/shard_map/stack | solution.py:46
  2278.5 85.5 %pad_maximum_fusion.1 = f32[2,8192,2048]{2,1,0:T(8,128)} fusion(f32[1,8192,2048]{2,1,0:T(8,128)} %get-tuple-element.8, f32[1,8192,2048]{2,1,0:T(8,128)} %get-tuple-element.7), kind=kLoop, calls=%fused_computation.1 | loop fusion | flops 33554432 | bytes 268435456 | tf_op jit(solution)/shard_map/stack | solution.py:46
  (11 shorter events, 0.0 us)
Async XLA Ops:
  7.2 1843.8 %all-reduce.6.cloned.1.call-start = ((), (), s32[]{:S(2)}) async-start(), calls=%async_computation.1 | async-start | bytes 201326592 | tf_op jit(solution)/shard_map/psum | solution.py:40
  7.9 15.8 copy-start.2
  303.5 2.6 copy-start.7
  379.6 77.7 %copy-start.3 = (bf16[3,512]{1,0:T(4,128)(2,1)S(1)}, bf16[3,512]{1,0:T(4,128)(2,1)}, u32[]{:S(2)}) copy-start(bf16[3,512]{1,0:T(4,128)(2,1)} %copy-done.2) | copy-start | bytes 9220
  525.3 79.3 %copy-start.6 = (bf16[3,512,2048]{2,1,0:T(8,128)(2,1)S(1)}, bf16[3,512,2048]{2,1,0:T(8,128)(2,1)}, u32[]{:S(2)}) copy-start(bf16[3,512,2048]{2,1,0:T(8,128)(2,1)} %fusion.117) | copy-start | bytes 18874372
  525.3 84.4 %copy-start.5 = (f32[2]{0:T(128)S(1)}, f32[2]{0:T(128)}, u32[]{:S(2)}) copy-start(f32[2]{0:T(128)} %param.15) | copy-start | bytes 28
  525.3 85.1 %copy-start.1 = (u8[512,8192]{1,0:T(8,128)(4,1)S(1)}, u8[512,8192]{1,0:T(8,128)(4,1)}, u32[]{:S(2)}) copy-start(u8[512,8192]{1,0:T(8,128)(4,1)} %get-tuple-element.15) | copy-start | bytes 12582916
  724.4 22.7 copy-start.9
  773.9 62.6 %copy-start = (bf16[3,512,2048]{2,1,0:T(8,128)(2,1)S(1)}, bf16[3,512,2048]{2,1,0:T(8,128)(2,1)}, u32[]{:S(2)}) copy-start(bf16[3,512,2048]{2,1,0:T(8,128)(2,1)} %param.9) | copy-start | bytes 18874372
  773.9 62.6 %copy-start.4 = (bf16[3,512]{1,0:T(4,128)(2,1)S(1)}, bf16[3,512]{1,0:T(4,128)(2,1)}, u32[]{:S(2)}) copy-start(bf16[3,512]{1,0:T(4,128)(2,1)} %copy-done.2) | copy-start | bytes 9220
  836.6 64.9 %copy-start.8 = (f32[3,512,512]{2,1,0:T(8,128)S(1)}, f32[3,512,512]{2,1,0:T(8,128)}, u32[]{:S(2)}) copy-start(f32[3,512,512]{2,1,0:T(8,128)} %fusion.140) | copy-start | bytes 9437188
  989.8 1183.6 %all-reduce.4.cloned.1.call-start = ((), (), s32[]{:S(2)}) async-start(), calls=%async_computation | async-start | bytes 67108864 | tf_op jit(solution)/shard_map/psum | solution.py:40
Sparse Core Ops, SparseCore 0:
  989.9 860.9 all-reduce.5
  1856.6 316.7 all-reduce.3
where the time goes:
time: 2380 us; the launch traced here: 2370 us
  matrix products  807 us (34%)
  other arithmetic  617 us (26%)
  waiting for transfers between devices  591 us (25%)
  local copies, waits for them, and re-layouts  341 us (14%)
    psum x2, waiting for transfers between devices, per_device(): lax.psum((up_part.astype(jnp.bfloat16), down_part.astype(jnp.bfloat16)),...  591 us
    another operation x4, other arithmetic, per_device(): return (jnp.stack(up_grads), jnp.stack(down_grads))  381 us
    unnamed x23, local copies, waits for them, and re-layouts  256 us
    convert_element_type x2, other arithmetic, per_device(): jax.nn.gelu(hidden.astype(jnp.float32), approximate=False)  228 us
    dot_general x2, matrix products, per_device(): jnp.einsum('btd,fd->btf', grad_cur, w_down[layer_idx], preferred_element_...  157 us
    dot_general x2, matrix products, per_device(): jnp.einsum('btd,df->btf', x_cur, w_up[layer_idx], preferred_element_type=...  135 us
    dot_general x2, matrix products, per_device(): jnp.einsum('btf,btd->fd', gelu_out, (grad_cur * factor).astype(jnp.bfloat...  128 us
    dot_general x8, matrix products, gram_of(): jnp.einsum('btk,bsk->bts', matrix, matrix, preferred_element_type=jnp.flo...  127 us
  transfers between devices with their start and end apart: 2, of which 2 were waited for; matrix products, arithmetic and copies ran while one was open for 25% of the time, Pallas kernels for 0%

commit v1 on v0

v1 whole, which is shorter than its diff:
```python
import functools
import jax
import jax.numpy as jnp
from jax import lax
from jax.experimental import pallas as pl
from jax.experimental.pallas import tpu as pltpu
from jax.sharding import PartitionSpec as P

F32 = jnp.float32
BF16 = jnp.bfloat16
MESH_ID = pl.DeviceIdType.MESH
ANY = pl.BlockSpec(memory_space=pl.ANY)
CW = 256
PER_MAT = 16
CHUNKS = 2 * PER_MAT
LAG1, LAG2, LAG3 = 4, 7, 10
RECV = 6
OWN = 10


def normal_cdf(z):
    return 0.5 * (1.0 + lax.erf(z * 0.7071067811865476))


def dot_nt(a, b):
    return lax.dot_general(a, b, (((1,), (1,)), ((), ())), preferred_element_type=F32)


def up_kernel(x_ref, w_ref, z_ref, a_ref):
    for start in range(0, x_ref.shape[0], 512):
        rows = pl.ds(start, 512)
        z = jnp.dot(x_ref[rows, :], w_ref[0], preferred_element_type=F32).astype(BF16)
        z_ref[rows, :] = z
        zf = z.astype(F32)
        a_ref[rows, :] = (zf * normal_cdf(zf)).astype(BF16)


def forward_up(layer, x_rows, w_up):
    n_rows, dim = x_rows.shape
    ff = w_up.shape[2]
    tile = 512
    out = jax.ShapeDtypeStruct((n_rows, ff), BF16)
    col = pl.BlockSpec((n_rows, tile), lambda j: (0, j))
    return pl.pallas_call(
        up_kernel, out_shape=(out, out), grid=(ff // tile,),
        in_specs=[pl.BlockSpec((n_rows, dim), lambda j: (0, 0)), pl.BlockSpec((1, dim, tile), lambda j: (layer, 0, j))],
        out_specs=(col, col), name='forward_up',
        cost_estimate=pl.CostEstimate(flops=2 * n_rows * dim * ff, bytes_accessed=dim * ff * 2 + n_rows * ff * 4, transcendentals=n_rows * ff),
        compiler_params=pltpu.CompilerParams(vmem_limit_bytes=56 * 1024 * 1024))(x_rows, w_up)


def add_kernel(transposed, a_ref, w_ref, x_ref, o_ref, acc):
    k = pl.program_id(1)

    @pl.when(k == 0)
    def _():
        acc[...] = x_ref[...].astype(F32)

    for start in range(0, a_ref.shape[0], 512):
        rows = pl.ds(start, 512)
        if transposed:
            acc[rows, :] += dot_nt(a_ref[rows, :], w_ref[0])
        else:
            acc[rows, :] += jnp.dot(a_ref[rows, :], w_ref[0], preferred_element_type=F32)

    @pl.when(k == pl.num_programs(1) - 1)
    def _():
        o_ref[...] = acc[...].astype(BF16)


def add_product(layer, x_rows, a_rows, weight, transposed):
    n_rows, dim = x_rows.shape
    ff = a_rows.shape[1]
    tn, tk = 1024, 2048
    if transposed:
        w_spec = pl.BlockSpec((1, tn, tk), lambda n, k: (layer, n, k))
    else:
        w_spec = pl.BlockSpec((1, tk, tn), lambda n, k: (layer, k, n))
    col = pl.BlockSpec((n_rows, tn), lambda n, k: (0, n))
    return pl.pallas_call(
        functools.partial(add_kernel, transposed), out_shape=jax.ShapeDtypeStruct((n_rows, dim), BF16), grid=(dim // tn, ff // tk),
        in_specs=[pl.BlockSpec((n_rows, tk), lambda n, k: (0, k)), w_spec, col],
        out_specs=col, scratch_shapes=[pltpu.VMEM((n_rows, tn), F32)], name='add_product',
        cost_estimate=pl.CostEstimate(flops=2 * n_rows * dim * ff, bytes_accessed=dim * ff * 2 + n_rows * ff * 4, transcendentals=0),
        compiler_params=pltpu.CompilerParams(vmem_limit_bytes=60 * 1024 * 1024))(a_rows, weight, x_rows)


def grad_kernel(has_hidden, n_samples, clip_ref, x_ref, g_ref, *refs):
    if has_hidden:
        z_ref, a_ref, wd_ref, h_ref, f_ref, gram_a, gram_h = refs
    else:
        wu_ref, wd_ref, a_ref, h_ref, f_ref, gram_a, gram_h = refs
    j = pl.program_id(0)
    seq = x_ref.shape[0] // n_samples
    half = seq // 2
    low, high = slice(0, half), slice(half, seq)

    @pl.when(j == 0)
    def _():
        gram_a[...] = jnp.zeros_like(gram_a)
        gram_h[...] = jnp.zeros_like(gram_h)

    for s in range(n_samples):
        rows = pl.ds(s * seq, seq)
        if has_hidden:
            z = z_ref[rows, :].astype(F32)
        else:
            z = jnp.dot(x_ref[rows, :], wu_ref[0], preferred_element_type=F32).astype(BF16).astype(F32)
        u = dot_nt(g_ref[rows, :], wd_ref[0])
        cdf = normal_cdf(z)
        if has_hidden:
            a = a_ref[rows, :]
        else:
            a = (z * cdf).astype(BF16)
            a_ref[rows, :] = a
        h = (u * (cdf + z * jnp.exp(-0.5 * z * z) * 0.3989422804014327)).astype(BF16)
        h_ref[rows, :] = h
        gram_a[s, low, low] += dot_nt(a[low], a[low])
        gram_a[s, high, :] += dot_nt(a[high], a)
        gram_h[s, low, low] += dot_nt(h[low], h[low])
        gram_h[s, high, :] += dot_nt(h[high], h)

    @pl.when(j == pl.num_programs(0) - 1)
    def _():
        for s in range(n_samples):
            first, second = pl.ds(s * seq, half), pl.ds(s * seq + half, half)

            def paired(r, rr, c, cc):
                gg = dot_nt(g_ref[rr, :], g_ref[cc, :])
                xx = dot_nt(x_ref[rr, :], x_ref[cc, :])
                return gram_a[s, r, c] * gg + gram_h[s, r, c] * xx

            total = paired(low, first, low, first) + paired(high, second, high, second) + 2.0 * paired(high, second, low, first)
            norm_sq = jnp.sum(total, axis=(0, 1), keepdims=True)
            factor = jnp.minimum(1.0, clip_ref[0] / jnp.sqrt(norm_sq))
            f_ref[pl.ds(s * seq, seq), :] = jnp.broadcast_to(factor, (seq, 1))


def block_grad(layer, x_rows, g_rows, hidden, w_up, w_down, clip, n_samples):
    n_rows, dim = x_rows.shape
    ff = w_up.shape[2]
    tile = 512
    seq = n_rows // n_samples
    col = pl.BlockSpec((n_rows, tile), lambda j: (0, j))
    whole = pl.BlockSpec((n_rows, dim), lambda j: (0, 0), pipeline_mode=pl.Buffered(buffer_count=1))
    wd_spec = pl.BlockSpec((1, tile, dim), lambda j: (layer, j, 0))
    rows_spec = pl.BlockSpec((n_rows, 1), lambda j: (0, 0))
    big = jax.ShapeDtypeStruct((n_rows, ff), BF16)
    row_out = jax.ShapeDtypeStruct((n_rows, 1), F32)
    smem = pl.BlockSpec(memory_space=pltpu.SMEM)
    products = 2 if hidden is None else 1
    if hidden is None:
        in_specs = [smem, whole, whole, pl.BlockSpec((1, dim, tile), lambda j: (layer, 0, j)), wd_spec]
        args = (clip, x_rows, g_rows, w_up, w_down)
        out_shape, out_specs = (big, big, row_out), (col, col, rows_spec)
    else:
        in_specs = [smem, whole, whole, col, col, wd_spec]
        args = (clip, x_rows, g_rows, hidden[0], hidden[1], w_down)
        out_shape, out_specs = (big, row_out), (col, rows_spec)
    return pl.pallas_call(
        functools.partial(grad_kernel, hidden is not None, n_samples), out_shape=out_shape, grid=(ff // tile,), in_specs=in_specs, out_specs=out_specs,
        scratch_shapes=[pltpu.VMEM((n_samples, seq, seq), F32)] * 2, name='block_grad',
        cost_estimate=pl.CostEstimate(flops=(2 * products * dim + 3 * seq) * n_rows * ff, bytes_accessed=dim * ff * 4 + n_rows * ff * 4, transcendentals=2 * n_rows * ff),
        compiler_params=pltpu.CompilerParams(vmem_limit_bytes=60 * 1024 * 1024))(*args)


def axis_weight(axis):
    return 2 * (axis + 1) + 2 * (axis // 2)


def sums_kernel(shift, x_hbm, h_hbm, a_hbm, g_hbm, rowf, r_hbm, lt, slab, gpiece, clip, own, s0s, s0r, rc1, rc2, rc3, obuf,
                slab_sem, g_sem, o_sem, d_send, d_recv, sems_s, sems_r):
    me = lax.axis_index('data')
    core = me % 2
    partner = me + 1 - 2 * core

    def bit_peer(chunk, stage):
        axis = (chunk + shift + stage) % 3
        weight = axis_weight(axis)
        bit = (me // weight) % 2
        return bit, me + weight * (1 - 2 * bit)

    barrier = pltpu.get_barrier_semaphore()
    pl.semaphore_signal(barrier, inc=1, device_id=(partner,), device_id_type=MESH_ID)
    for axis in range(3):
        weight = axis_weight(axis)
        peer = me + weight * (1 - 2 * ((me // weight) % 2))
        pl.semaphore_signal(barrier, inc=1, device_id=(peer,), device_id_type=MESH_ID)
    pl.semaphore_wait(barrier, 4)

    def columns(half, chunk):
        return pl.ds(pl.multiple_of((half * PER_MAT + chunk % PER_MAT) * CW, CW), CW)

    def start_slab(half, chunk, buf):
        @pl.when(chunk < PER_MAT)
        def _():
            pltpu.make_async_copy(h_hbm.at[:, columns(half, chunk)], slab.at[buf], slab_sem.at[buf]).start()

        @pl.when(chunk >= PER_MAT)
        def _():
            pltpu.make_async_copy(a_hbm.at[:, columns(half, chunk)], slab.at[buf], slab_sem.at[buf]).start()

    def wait_slab(buf):
        pltpu.make_async_copy(h_hbm.at[:, pl.ds(0, CW)], slab.at[buf], slab_sem.at[buf]).wait()

    def x_copy(piece):
        return pltpu.make_async_copy(x_hbm.at[:, pl.ds(piece * CW, CW)], slab.at[piece % 4], slab_sem.at[piece % 4])

    n_pieces = x_hbm.shape[1] // CW
    for piece in range(3):
        x_copy(piece).start()
    for piece in range(n_pieces):
        if piece + 3 < n_pieces:
            x_copy(piece + 3).start()
        x_copy(piece).wait()
        lt[0, pl.ds(piece * CW, CW), :] = slab[piece % 4].T

    def g_copy(piece):
        return pltpu.make_async_copy(g_hbm.at[:, pl.ds(pl.multiple_of(piece * CW, CW), CW)], gpiece, g_sem)

    def load_clip(chunk, buf):
        scale = jnp.where(chunk < PER_MAT, rowf[...], 1.0)
        clip[...] = (slab[buf].astype(F32) * scale).astype(BF16)

    def partner_chunk(chunk):
        buf = chunk % 2
        wait_slab(buf)
        load_clip(chunk, buf)

        @pl.when(chunk + 1 < CHUNKS)
        def _():
            start_slab(1 - core, chunk + 1, 1 - buf)

        mat = chunk // PER_MAT
        for q in range(4):
            rows = pl.ds(q * 512, 512)
            s0s[buf, rows, :] = jnp.dot(lt[mat, rows, :], clip[...], preferred_element_type=F32).astype(BF16)

    def d2d(chunk):
        buf = chunk % 2
        return pltpu.make_async_remote_copy(s0s.at[buf], s0r.at[buf], d_send.at[buf], d_recv.at[buf], device_id=(partner,), device_id_type=MESH_ID)

    def own_chunk(chunk):
        buf = 2 + chunk % 2
        wait_slab(buf)
        load_clip(chunk, buf)

        @pl.when(chunk + 1 < CHUNKS)
        def _():
            start_slab(core, chunk + 1, 5 - buf)

        d2d(chunk).wait()
        mat = chunk // PER_MAT
        for q in range(4):
            rows = pl.ds(q * 512, 512)
            part = jnp.dot(lt[mat, rows, :], clip[...], preferred_element_type=F32)
            own[chunk % OWN, rows, :] = (part + s0r[chunk % 2, rows, :].astype(F32)).astype(BF16)

    def kept_row(chunk, stage):
        row = 0
        for s in range(stage):
            bit, _ = bit_peer(chunk, s)
            row = row + bit * (1024 // (2 ** s))
        return row

    recv_bufs = (rc1, rc2, rc3)

    def stage_copy(chunk, stage):
        size = 1024 // (2 ** stage)
        bit, peer = bit_peer(chunk, stage)
        row = kept_row(chunk, stage) + (1 - bit) * size
        slot = chunk % RECV
        return pltpu.make_async_remote_copy(
            own.at[chunk % OWN, pl.ds(pl.multiple_of(row, CW), size), :], recv_bufs[stage].at[slot],
            sems_s.at[stage, slot], sems_r.at[stage, slot], device_id=(peer,), device_id_type=MESH_ID)

    def stage_sum(chunk, stage):
        size = 1024 // (2 ** stage)
        rows = pl.ds(pl.multiple_of(kept_row(chunk, stage + 1), CW), size)
        return rows, own[chunk % OWN, rows, :].astype(F32) + recv_bufs[stage][chunk % RECV].astype(F32)

    def out_copy(chunk):
        return pltpu.make_async_copy(obuf.at[chunk % 2], r_hbm.at[chunk], o_sem.at[chunk % 2])

    start_slab(1 - core, 0, 0)
    start_slab(core, 0, 2)
    partner_chunk(0)
    g_copy(0).start()
    d2d(0).start()

    def step(t, _):
        @pl.when(t >= LAG3)
        def _():
            chunk = t - LAG3
            stage_copy(chunk, 2).wait()
            _, total = stage_sum(chunk, 2)

            @pl.when(chunk >= 2)
            def _():
                out_copy(chunk - 2).wait()

            @pl.when(chunk < PER_MAT)
            def _():
                obuf[chunk % 2] = total.astype(BF16)

            @pl.when(chunk >= PER_MAT)
            def _():
                obuf[chunk % 2] = total.T.astype(BF16)

            out_copy(chunk).start()

        @pl.when((t >= LAG2) & (t < CHUNKS + LAG2))
        def _():
            chunk = t - LAG2
            stage_copy(chunk, 1).wait()
            rows, total = stage_sum(chunk, 1)
            own[chunk % OWN, rows, :] = total.astype(BF16)

        @pl.when((t >= LAG1) & (t < CHUNKS + LAG1))
        def _():
            chunk = t - LAG1
            stage_copy(chunk, 0).wait()
            rows, total = stage_sum(chunk, 0)
            own[chunk % OWN, rows, :] = total.astype(BF16)

        @pl.when((t >= 1) & (t < CHUNKS + 1))
        def _():
            stage_copy(t - 1, 0).start()

        @pl.when(t < n_pieces)
        def _():
            g_copy(t).wait()
            lt[1, pl.ds(pl.multiple_of(t * CW, CW), CW), :] = (gpiece[...].astype(F32) * rowf[...]).astype(BF16).T

            @pl.when(t + 1 < n_pieces)
            def _():
                g_copy(t + 1).start()

        @pl.when(t < CHUNKS - 1)
        def _():
            partner_chunk(t + 1)

        @pl.when(t < CHUNKS)
        def _():
            own_chunk(t)

        @pl.when(t < CHUNKS - 1)
        def _():
            d2d(t + 1).start()

        @pl.when((t >= LAG1) & (t < CHUNKS + LAG1))
        def _():
            stage_copy(t - LAG1, 1).start()

        @pl.when((t >= LAG2) & (t < CHUNKS + LAG2))
        def _():
            stage_copy(t - LAG2, 2).start()

        return 0

    lax.fori_loop(0, CHUNKS + LAG3, step, 0)
    out_copy(CHUNKS - 2).wait()
    out_copy(CHUNKS - 1).wait()


def block_sums(layer, x_rows, h_rows, a_rows, g_rows, row_factor):
    n_rows, dim = x_rows.shape
    scratch = [
        pltpu.VMEM((2, dim, n_rows), BF16), pltpu.VMEM((4, n_rows, CW), BF16), pltpu.VMEM((n_rows, CW), BF16), pltpu.VMEM((n_rows, CW), BF16),
        pltpu.VMEM((OWN, dim, CW), BF16), pltpu.VMEM((2, dim, CW), BF16), pltpu.VMEM((2, dim, CW), BF16),
        pltpu.VMEM((RECV, dim // 2, CW), BF16), pltpu.VMEM((RECV, dim // 4, CW), BF16), pltpu.VMEM((RECV, dim // 8, CW), BF16),
        pltpu.VMEM((2, CW, CW), BF16),
        pltpu.SemaphoreType.DMA((4,)), pltpu.SemaphoreType.DMA, pltpu.SemaphoreType.DMA((2,)),
        pltpu.SemaphoreType.DMA((2,)), pltpu.SemaphoreType.DMA((2,)), pltpu.SemaphoreType.DMA((3, RECV)), pltpu.SemaphoreType.DMA((3, RECV)),
    ]
    flops = 4 * n_rows * dim * h_rows.shape[1]
    return pl.pallas_call(
        functools.partial(sums_kernel, 2 * layer),
        out_shape=jax.ShapeDtypeStruct((CHUNKS, CW, CW), BF16),
        in_specs=[ANY, ANY, ANY, ANY, pl.BlockSpec(memory_space=pltpu.VMEM)],
        out_specs=ANY,
        scratch_shapes=scratch,
        compiler_params=pltpu.CompilerParams(collective_id=layer, has_side_effects=True, vmem_limit_bytes=60 * 1024 * 1024),
        cost_estimate=pl.CostEstimate(flops=flops, bytes_accessed=4 * n_rows * h_rows.shape[1], transcendentals=0),
        name=f'sums_{layer}',
    )(x_rows, h_rows, a_rows, g_rows, row_factor)


def owner_of(chunk, piece, half, shift):
    color = (chunk + shift) % 3
    b1, b2, b3 = piece // 4, (piece // 2) % 2, piece % 2
    return b1 * axis_weight(color) + b2 * axis_weight((color + 1) % 3) + b3 * axis_weight((color + 2) % 3) + half


def finish_kernel(n_in, scale, *refs):
    pieces, noise, out = refs[:n_in], refs[n_in], refs[-1]
    for i in range(n_in):
        cols = pl.ds(i * CW, CW)
        out[0, :, cols] = (pieces[i][0, 0].astype(F32) + noise[0, :, cols]) * scale


def finish_up(layer, gathered, noise, prev, batch_total):
    layers, dim, ff = noise.shape
    shift = 2 * layer

    def piece_spec(c):
        return pl.BlockSpec((1, 1, CW, CW), lambda i, k, c=c: (owner_of(c, i, k, shift), c, 0, 0))

    tile = pl.BlockSpec((1, CW, ff // 2), lambda i, k: (layer, i, k))
    in_specs = [piece_spec(c) for c in range(PER_MAT)] + [tile]
    args = [gathered] * PER_MAT + [noise]
    aliases = {}
    if prev is not None:
        in_specs.append(ANY)
        args.append(prev)
        aliases = {len(args) - 1: 0}
    return pl.pallas_call(
        functools.partial(finish_kernel, PER_MAT, 1.0 / batch_total),
        out_shape=jax.ShapeDtypeStruct(noise.shape, F32), grid=(dim // CW, 2), in_specs=in_specs, out_specs=tile,
        input_output_aliases=aliases, name=f'finish_up_{layer}',
        cost_estimate=pl.CostEstimate(flops=dim * ff * 2, bytes_accessed=dim * ff * 10, transcendentals=0),
        compiler_params=pltpu.CompilerParams(vmem_limit_bytes=50 * 1024 * 1024))(*args)


def finish_down(layer, gathered, noise, prev, batch_total):
    layers, ff, dim = noise.shape
    shift = 2 * layer
    n_in = dim // CW

    def piece_spec(i):
        return pl.BlockSpec((1, 1, CW, CW), lambda k, c, i=i: (owner_of(c + PER_MAT, i, k, shift), c + PER_MAT, 0, 0))

    tile = pl.BlockSpec((1, CW, dim), lambda k, c: (layer, k * PER_MAT + c, 0))
    in_specs = [piece_spec(i) for i in range(n_in)] + [tile]
    args = [gathered] * n_in + [noise]
    aliases = {}
    if prev is not None:
        in_specs.append(ANY)
        args.append(prev)
        aliases = {len(args) - 1: 0}
    return pl.pallas_call(
        functools.partial(finish_kernel, n_in, 1.0 / batch_total),
        out_shape=jax.ShapeDtypeStruct(noise.shape, F32), grid=(2, PER_MAT), in_specs=in_specs, out_specs=tile,
        input_output_aliases=aliases, name=f'finish_down_{layer}',
        cost_estimate=pl.CostEstimate(flops=dim * ff * 2, bytes_accessed=dim * ff * 10, transcendentals=0),
        compiler_params=pltpu.CompilerParams(vmem_limit_bytes=50 * 1024 * 1024))(*args)


def per_device(x_in, dy_out, lengths, w_up, w_down, noise_up, noise_down, clip_norm, batch_total):
    n_samples, seq_len, dim = x_in.shape
    n_rows = n_samples * seq_len
    tok_mask = (jnp.arange(seq_len)[None, :] < lengths[:, None]).astype(BF16)
    g_last = (dy_out * tok_mask[:, :, None]).reshape(n_rows, dim)
    x_first = x_in.reshape(n_rows, dim)
    z_first, a_first = forward_up(0, x_first, w_up)
    x_last = add_product(0, x_first, a_first, w_down, False)
    a_last, h_last, row_factor = block_grad(1, x_last, g_last, None, w_up, w_down, clip_norm[1:], n_samples)
    piece = block_sums(1, x_last, h_last, a_last, g_last, row_factor)
    gathered = lax.all_gather(piece, 'data')
    g_first = add_product(1, g_last, h_last, w_up, True)
    h_first, row_factor = block_grad(0, x_first, g_first, (z_first, a_first), w_up, w_down, clip_norm[:1], n_samples)
    piece = block_sums(0, x_first, h_first, a_first, g_first, row_factor)
    gathered_first = lax.all_gather(piece, 'data')
    grad_up = finish_up(1, gathered, noise_up, None, batch_total)
    grad_down = finish_down(1, gathered, noise_down, None, batch_total)
    grad_up = finish_up(0, gathered_first, noise_up, grad_up, batch_total)
    grad_down = finish_down(0, gathered_first, noise_down, grad_down, batch_total)
    return grad_up, grad_down


def solution(mesh):
    batch_spec = P('data', None, None)

    def grad_step(x_in, dy_out, lengths, w_up, w_down, noise_up, noise_down, clip_norm):
        device_fn = functools.partial(per_device, batch_total=x_in.shape[0])
        mapped = jax.shard_map(device_fn, mesh=mesh, in_specs=(batch_spec, batch_spec, P('data'), P(), P(), P(), P(), P()), out_specs=(P(), P()), check_vma=False)
        return mapped(x_in, dy_out, lengths, w_up, w_down, noise_up, noise_down, clip_norm)

    return grad_step
```

time: 2380 us -> 1360 us (0.57)
  Pallas kernels: 0 us -> 1200 us
  matrix products: 807 us -> 0 us
  other arithmetic: 617 us -> 6.73 us
  waiting for transfers between devices: 591 us -> 126 us
  local copies, waits for them, and re-layouts: 341 us -> 1.38 us
    pallas_call x0 -> x11, Pallas kernels: none -> 1200 us  [the longest x2 534 us: block_sums(): pl.pallas_call(functools.partial(sums_kernel, 2 * layer), out_shape=jax.S...]
    dot_general x18 -> x0, matrix products: 807 us -> none  [the longest x2 157 us: per_device(): jnp.einsum('btd,fd->btf', grad_cur, w_down[layer_idx], preferred_element_...]
    psum x2 -> x0, waiting for transfers between devices: 591 us -> none  [per_device(): lax.psum((up_part.astype(jnp.bfloat16), down_part.astype(jnp.bfloat16)),...]
    another operation x4 -> x0, other arithmetic: 381 us -> none  [per_device(): return (jnp.stack(up_grads), jnp.stack(down_grads))]
    unnamed x23 -> x0, local copies, waits for them, and re-layouts: 256 us -> none
    convert_element_type x3 -> x1, other arithmetic: 229 us -> 0.73 us  [per_device(): tok_mask = (jnp.arange(seq_len)[None, :] < lengths[:, None]).astype(BF16)]
    all_gather x0 -> x2, waiting for transfers between devices: none -> 126 us  [the longest x1 126 us: per_device(): gathered_first = lax.all_gather(piece, 'data')]
    slice x2 -> x1, local copies, waits for them, and re-layouts: 85.1 us -> 1.38 us  [per_device(): clip_norm[1:]]
  transfers between devices with their start and end apart: 2 -> 2, of which waited for: 2 -> 1; matrix products, arithmetic and copies ran while one was open for 25% -> 0% of each run, Pallas kernels for 0% -> 42%
where the time goes in v1:
time: 1360 us; the launch traced here: 1350 us
  Pallas kernels  1200 us (88%)
  waiting for transfers between devices  126 us (9%)
  between operations  14.5 us (1%)
    pallas_call x2, Pallas kernels, block_sums(): pl.pallas_call(functools.partial(sums_kernel, 2 * layer), out_shape=jax.S...  534 us
    pallas_call x2, Pallas kernels, block_grad(): pl.pallas_call(functools.partial(grad_kernel, hidden is not None, n_sampl...  245 us
    all_gather x1, waiting for transfers between devices, per_device(): gathered_first = lax.all_gather(piece, 'data')  126 us
    pallas_call x2, Pallas kernels, add_product(): pl.pallas_call(functools.partial(add_kernel, transposed), out_shape=jax.S...  124 us
    pallas_call x2, Pallas kernels, finish_down(): pl.pallas_call(functools.partial(finish_kernel, n_in, 1.0 / batch_total),...  123 us
    pallas_call x2, Pallas kernels, finish_up(): pl.pallas_call(functools.partial(finish_kernel, PER_MAT, 1.0 / batch_tota...  108 us
    pallas_call x1, Pallas kernels, forward_up(): pl.pallas_call(up_kernel, out_shape=(out, out), grid=(ff // tile,), in_sp...  67.6 us
  transfers between devices with their start and end apart: 2, of which 1 were waited for; matrix products, arithmetic and copies ran while one was open for 0% of the time, Pallas kernels for 42%

profile of v1, /device:TPU:0, one launch (start us, length us, event | category | flops | bytes accessed | tf_op | source)
XLA Modules:
  0.0 1349.6 jit_solution(14460821586853895349)
XLA Ops:
  7.2 0.0 all-gather.7.cloned.1.call-start
  7.2 1.4 fusion.1
  8.6 0.7 fusion
  9.3 6.0 broadcast_multiply_fusion
  15.3 67.6 %forward_up.1 = (bf16[1536,8192]{1,0:T(8,128)(2,1)}, bf16[1536,8192]{1,0:T(8,128)(2,1)}) custom-call(bf16[1536,2048]{1,0:T(8,128)(2,1)} %bitcast.7, bf16[2,2048,8192]{2,1,0:T(8,128)(2,1)} %w_ref.5), custom_call_target="tpu_custom_call" | custom-call | flops 51539607552 | bytes 83886080 | tf_op jit(solution)/shard_map/forward_up/pallas_call | solution.py:44
  82.9 61.7 %add_product.2.x_ref.x_hbm = bf16[1536,2048]{1,0:T(8,128)(2,1)} custom-call(bf16[1536,8192]{1,0:T(8,128)(2,1)} %get-tuple-element.9.a_ref.refs_1_.a_hbm, bf16[2,8192,2048]{2,1,0:T(8,128)(2,1)} %refs_2_.1, bf16[1536,2048]{1,0:T(8,128)(2,1)} %bitcast.8), custom_call_target="tpu_custom_call" | custom-call | flops 51539607552 | bytes 83886080 | tf_op jit(solution)/shard_map/add_product/pallas_call | solution.py:80
  144.6 146.3 %block_grad.2 = (bf16[1536,8192]{1,0:T(8,128)(2,1)}, bf16[1536,8192]{1,0:T(8,128)(2,1)}, f32[1536,1]{1,0:T(8,128)}) custom-call(f32[1]{0:T(128)} %get-tuple-element.16.clip_ref, bf16[1536,2048]{1,0:T(8,128)(2,1)} %add_product.2.x_ref.x_hbm, bf16[1536,2048]{1,0:T(8,128)(2,1)} %bitcast.4, bf16[2,2048,8192]{2,1,0:T(8,128)(2,1)} %w_ref.5, ...), custom_call_target="tpu_custom_call" | custom-call | flops 122406567936 | bytes 117440512 | tf_op jit(solution)/shard_map/block_grad/pallas_call | solution.py:160
  290.8 242.6 %sums_1.1 = bf16[32,256,256]{2,1,0:T(8,128)(2,1)} custom-call(bf16[1536,2048]{1,0:T(8,128)(2,1)} %add_product.2.x_ref.x_hbm, bf16[1536,8192]{1,0:T(8,128)(2,1)} %get-tuple-element.10.a_ref.h_hbm, bf16[1536,8192]{1,0:T(8,128)(2,1)} %get-tuple-element.14.a_hbm, bf16[1536,2048]{1,0:T(8,128)(2,1)} %bitcast.5, f32[1536,1]{1,0:T(8,128)} %get-tuple-element.15.rowf), custom_call_target="tpu_custom_call" | custom-call | flops 103079215104 | bytes 50331648 | tf_op jit(solution)/shard_map/sums_1/pallas_call | solution.py:377
  533.4 0.0 all-gather.7.cloned.1.call-update
  533.4 0.0 all-gather.5.cloned.1.call-start
  533.5 62.0 %add_product.3.g_ref.g_hbm = bf16[1536,2048]{1,0:T(8,128)(2,1)} custom-call(bf16[1536,8192]{1,0:T(8,128)(2,1)} %get-tuple-element.10.a_ref.h_hbm, bf16[2,2048,8192]{2,1,0:T(8,128)(2,1)} %w_ref.5, bf16[1536,2048]{1,0:T(8,128)(2,1)} %bitcast.6), custom_call_target="tpu_custom_call" | custom-call | flops 51539607552 | bytes 83886080 | tf_op jit(solution)/shard_map/add_product/pallas_call | solution.py:80
  595.5 98.9 %block_grad.3 = (bf16[1536,8192]{1,0:T(8,128)(2,1)}, f32[1536,1]{1,0:T(8,128)}) custom-call(f32[1]{0:T(128)} %get-tuple-element.17.clip_ref, bf16[1536,2048]{1,0:T(8,128)(2,1)} %bitcast.9, bf16[1536,2048]{1,0:T(8,128)(2,1)} %add_product.3.g_ref.g_hbm, bf16[1536,8192]{1,0:T(8,128)(2,1)} %get-tuple-element.11.refs_0_, ...), custom_call_target="tpu_custom_call" | custom-call | flops 70866960384 | bytes 117440512 | tf_op jit(solution)/shard_map/block_grad/pallas_call | solution.py:160
  694.4 291.5 %sums_0.1 = bf16[32,256,256]{2,1,0:T(8,128)(2,1)} custom-call(bf16[1536,2048]{1,0:T(8,128)(2,1)} %bitcast.10, bf16[1536,8192]{1,0:T(8,128)(2,1)} %get-tuple-element.12.h_hbm, bf16[1536,8192]{1,0:T(8,128)(2,1)} %get-tuple-element.9.a_ref.refs_1_.a_hbm, bf16[1536,2048]{1,0:T(8,128)(2,1)} %add_product.3.g_ref.g_hbm, f32[1536,1]{1,0:T(8,128)} %get-tuple-element.13.rowf), custom_call_target="tpu_custom_call" | custom-call | flops 103079215104 | bytes 50331648 | tf_op jit(solution)/shard_map/sums_0/pallas_call | solution.py:377
  985.9 0.0 all-gather.5.cloned.1.call-update
  985.9 0.0 all-gather.7.cloned.1.call-done
  985.9 61.4 %finish_down_1.1.refs_9_ = f32[2,8192,2048]{2,1,0:T(8,128)} custom-call(bf16[16,32,256,256]{3,2,1,0:T(8,128)(2,1)} %bitcast.3.refs_0_.refs_1_.refs_2_.refs_3_.refs_4_.refs_5_.refs_6_.refs_7_.refs_8_.refs_9_.refs_10_.refs_11_.refs_12_.refs_13_.refs_14_.refs_15_, ...), custom_call_target="tpu_custom_call" | custom-call | flops 33554432 | bytes 167772160 | tf_op jit(solution)/shard_map/finish_down_1/pallas_call | solution.py:441
  1047.3 53.8 %finish_up_1.1.refs_17_ = f32[2,2048,8192]{2,1,0:T(8,128)} custom-call(bf16[16,32,256,256]{3,2,1,0:T(8,128)(2,1)} %bitcast.3.refs_0_.refs_1_.refs_2_.refs_3_.refs_4_.refs_5_.refs_6_.refs_7_.refs_8_.refs_9_.refs_10_.refs_11_.refs_12_.refs_13_.refs_14_.refs_15_, ...), custom_call_target="tpu_custom_call" | custom-call | flops 33554432 | bytes 167772160 | tf_op jit(solution)/shard_map/finish_up_1/pallas_call | solution.py:417
  1101.1 126.1 %all-gather.5.cloned.1.call-done = bf16[512,256,256]{2,1,0:T(8,128)(2,1)} async-done(((bf16[32,256,256]{2,1,0:T(8,128)(2,1)}), bf16[512,256,256]{2,1,0:T(8,128)(2,1)}) %all-gather.5.cloned.1.call-update) | async-done | bytes 67108880 | tf_op jit(solution)/shard_map/all_gather | solution.py:463
  1227.2 61.3 %finish_down_0.1 = f32[2,8192,2048]{2,1,0:T(8,128)} custom-call(bf16[16,32,256,256]{3,2,1,0:T(8,128)(2,1)} %bitcast.2.refs_0_.refs_1_.refs_2_.refs_3_.refs_4_.refs_5_.refs_6_.refs_7_.refs_8_.refs_9_.refs_10_.refs_11_.refs_12_.refs_13_.refs_14_.refs_15_, ...), custom_call_target="tpu_custom_call", output_to_operand_aliasing={{}: (9, {})} | custom-call | flops 33554432 | bytes 167772160 | tf_op jit(solution)/shard_map/finish_down_0/pallas_call | solution.py:441
  1288.5 53.8 %finish_up_0.1 = f32[2,2048,8192]{2,1,0:T(8,128)} custom-call(bf16[16,32,256,256]{3,2,1,0:T(8,128)(2,1)} %bitcast.2.refs_0_.refs_1_.refs_2_.refs_3_.refs_4_.refs_5_.refs_6_.refs_7_.refs_8_.refs_9_.refs_10_.refs_11_.refs_12_.refs_13_.refs_14_.refs_15_, ...), custom_call_target="tpu_custom_call", output_to_operand_aliasing={{}: (17, {})} | custom-call | flops 33554432 | bytes 167772160 | tf_op jit(solution)/shard_map/finish_up_0/pallas_call | solution.py:417
Async XLA Ops:
  7.2 978.7 %all-gather.7.cloned.1.call-start = ((), (), s32[]{:S(2)}) async-start(), calls=%async_computation.1 | async-start | bytes 71303168 | tf_op jit(solution)/shard_map/all_gather | solution.py:459
  533.4 693.8 %all-gather.5.cloned.1.call-start = ((), (), s32[]{:S(2)}) async-start(), calls=%async_computation | async-start | bytes 71303168 | tf_op jit(solution)/shard_map/all_gather | solution.py:463
Sparse Core Ops, SparseCore 0:
  533.6 296.3 all-gather.6
  986.0 241.1 all-gather.4

commit v2 on v1

v2 whole, which is shorter than its diff:
```python
import functools
import jax
import jax.numpy as jnp
from jax import lax
from jax.experimental import pallas as pl
from jax.experimental.pallas import tpu as pltpu
from jax.sharding import PartitionSpec as P

F32 = jnp.float32
BF16 = jnp.bfloat16
MESH_ID = pl.DeviceIdType.MESH
ANY = pl.BlockSpec(memory_space=pl.ANY)
CW = 256
PER_MAT = 16
CHUNKS = 2 * PER_MAT
SPLIT = 24
LAG1, LAG2, LAG3 = 4, 7, 10
RECV = 6
OWN = 10


def normal_cdf(z):
    return 0.5 * (1.0 + lax.erf(z * 0.7071067811865476))


def dot_nt(a, b):
    return lax.dot_general(a, b, (((1,), (1,)), ((), ())), preferred_element_type=F32)


def forward_kernel(block, x_ref, wu_ref, wd_ref, z_ref, a_ref, o_ref, acc):
    j = pl.program_id(0)

    @pl.when(j == 0)
    def _():
        acc[...] = x_ref[...].astype(F32)

    for start in range(0, x_ref.shape[0], block):
        rows = pl.ds(start, block)
        z = jnp.dot(x_ref[rows, :], wu_ref[0], preferred_element_type=F32).astype(BF16)
        z_ref[rows, :] = z
        zf = z.astype(F32)
        a = (zf * normal_cdf(zf)).astype(BF16)
        a_ref[rows, :] = a
        acc[rows, :] += jnp.dot(a, wd_ref[0], preferred_element_type=F32)

    @pl.when(j == pl.num_programs(0) - 1)
    def _():
        o_ref[...] = acc[...].astype(BF16)


def resident(shape):
    return pl.BlockSpec(shape, lambda j: (0, 0), pipeline_mode=pl.Buffered(buffer_count=1))


def forward_block(layer, x_rows, w_up, w_down):
    n_rows, dim = x_rows.shape
    ff = w_up.shape[2]
    tile = 512
    big = jax.ShapeDtypeStruct((n_rows, ff), BF16)
    col = pl.BlockSpec((n_rows, tile), lambda j: (0, j))
    return pl.pallas_call(
        functools.partial(forward_kernel, n_rows // 2), out_shape=(big, big, jax.ShapeDtypeStruct((n_rows, dim), BF16)), grid=(ff // tile,),
        in_specs=[resident((n_rows, dim)), pl.BlockSpec((1, dim, tile), lambda j: (layer, 0, j)), pl.BlockSpec((1, tile, dim), lambda j: (layer, j, 0))],
        out_specs=(col, col, resident((n_rows, dim))), scratch_shapes=[pltpu.VMEM((n_rows, dim), F32)], name='forward_block',
        cost_estimate=pl.CostEstimate(flops=4 * n_rows * dim * ff, bytes_accessed=dim * ff * 4 + n_rows * ff * 4, transcendentals=n_rows * ff),
        compiler_params=pltpu.CompilerParams(vmem_limit_bytes=63 * 1024 * 1024))(x_rows, w_up, w_down)


def add_kernel(transposed, a_ref, w_ref, x_ref, o_ref, acc):
    k = pl.program_id(1)

    @pl.when(k == 0)
    def _():
        acc[...] = x_ref[...].astype(F32)

    for start in range(0, a_ref.shape[0], 512):
        rows = pl.ds(start, 512)
        if transposed:
            acc[rows, :] += dot_nt(a_ref[rows, :], w_ref[0])
        else:
            acc[rows, :] += jnp.dot(a_ref[rows, :], w_ref[0], preferred_element_type=F32)

    @pl.when(k == pl.num_programs(1) - 1)
    def _():
        o_ref[...] = acc[...].astype(BF16)


def add_product(layer, x_rows, a_rows, weight, transposed):
    n_rows, dim = x_rows.shape
    ff = a_rows.shape[1]
    tn, tk = 1024, 2048
    if transposed:
        w_spec = pl.BlockSpec((1, tn, tk), lambda n, k: (layer, n, k))
    else:
        w_spec = pl.BlockSpec((1, tk, tn), lambda n, k: (layer, k, n))
    col = pl.BlockSpec((n_rows, tn), lambda n, k: (0, n))
    return pl.pallas_call(
        functools.partial(add_kernel, transposed), out_shape=jax.ShapeDtypeStruct((n_rows, dim), BF16), grid=(dim // tn, ff // tk),
        in_specs=[pl.BlockSpec((n_rows, tk), lambda n, k: (0, k)), w_spec, col],
        out_specs=col, scratch_shapes=[pltpu.VMEM((n_rows, tn), F32)], name='add_product',
        cost_estimate=pl.CostEstimate(flops=2 * n_rows * dim * ff, bytes_accessed=dim * ff * 2 + n_rows * ff * 4, transcendentals=0),
        compiler_params=pltpu.CompilerParams(vmem_limit_bytes=60 * 1024 * 1024))(a_rows, weight, x_rows)


def grad_kernel(first, n_samples, clip_ref, len_ref, x_ref, g_in, *refs):
    if first:
        g_ref = g_in
        z_ref, a_ref, wd_ref, h_ref, fr_ref, f_ref, xt_ref, gt_ref, gram_a, gram_h = refs
    else:
        wu_ref, wd_ref, a_ref, h_ref, fr_ref, f_ref, xt_ref, gt_ref, g_ref, gram_a, gram_h = refs
    j = pl.program_id(0)
    seq = x_ref.shape[0] // n_samples
    half = seq // 2
    low, high = slice(0, half), slice(half, seq)

    @pl.when(j == 0)
    def _():
        gram_a[...] = jnp.zeros_like(gram_a)
        gram_h[...] = jnp.zeros_like(gram_h)
        if not first:
            for s in range(n_samples):
                rows = pl.ds(s * seq, seq)
                valid = lax.broadcasted_iota(jnp.int32, (seq, 1), 0) < len_ref[s]
                g_ref[rows, :] = jnp.where(valid, g_in[rows, :].astype(F32), 0.0).astype(BF16)

    width = xt_ref.shape[0]
    cols = pl.ds(pl.multiple_of(j * width, width), width)
    xt_ref[...] = x_ref[:, cols].T
    gt_ref[...] = g_ref[:, cols].T
    for s in range(n_samples):
        rows = pl.ds(s * seq, seq)
        if first:
            z = z_ref[rows, :].astype(F32)
        else:
            z = jnp.dot(x_ref[rows, :], wu_ref[0], preferred_element_type=F32).astype(BF16).astype(F32)
        u = dot_nt(g_ref[rows, :], wd_ref[0])
        cdf = normal_cdf(z)
        if first:
            a = a_ref[rows, :]
        else:
            a = (z * cdf).astype(BF16)
            a_ref[rows, :] = a
        h = (u * (cdf + z * jnp.exp(-0.5 * z * z) * 0.3989422804014327)).astype(BF16)
        h_ref[rows, :] = h
        gram_a[s, low, low] += dot_nt(a[low], a[low])
        gram_a[s, high, :] += dot_nt(a[high], a)
        gram_h[s, low, low] += dot_nt(h[low], h[low])
        gram_h[s, high, :] += dot_nt(h[high], h)

    @pl.when(j == pl.num_programs(0) - 1)
    def _():
        for s in range(n_samples):
            first_half, second_half = pl.ds(s * seq, half), pl.ds(s * seq + half, half)

            def paired(r, rr, c, cc):
                gg = dot_nt(g_ref[rr, :], g_ref[cc, :])
                xx = dot_nt(x_ref[rr, :], x_ref[cc, :])
                return gram_a[s, r, c] * gg + gram_h[s, r, c] * xx

            total = (paired(low, first_half, low, first_half) + paired(high, second_half, high, second_half)
                     + 2.0 * paired(high, second_half, low, first_half))
            norm_sq = jnp.sum(total, axis=(0, 1), keepdims=True)
            factor = jnp.minimum(1.0, clip_ref[0] / jnp.sqrt(norm_sq))
            f_ref[:, pl.ds(s * seq, seq)] = jnp.broadcast_to(factor, (1, seq))
            fr_ref[pl.ds(s * seq, seq), :] = jnp.broadcast_to(factor, (seq, 1))


def block_grad(layer, x_rows, g_rows, hidden, w_up, w_down, clip, lengths):
    n_rows, dim = x_rows.shape
    n_samples = lengths.shape[0]
    ff = w_up.shape[2]
    tile = 512
    steps = ff // tile
    seq = n_rows // n_samples
    col = pl.BlockSpec((n_rows, tile), lambda j: (0, j))
    whole = resident((n_rows, dim))
    wd_spec = pl.BlockSpec((1, tile, dim), lambda j: (layer, j, 0))
    big = jax.ShapeDtypeStruct((n_rows, ff), BF16)
    f_out = (jax.ShapeDtypeStruct((n_rows, 1), F32), jax.ShapeDtypeStruct((1, n_rows), F32))
    f_spec = (resident((n_rows, 1)), resident((1, n_rows)))
    turned, t_spec = jax.ShapeDtypeStruct((dim, n_rows), BF16), pl.BlockSpec((dim // steps, n_rows), lambda j: (j, 0))
    smem = pl.BlockSpec(memory_space=pltpu.SMEM)
    first = hidden is not None
    if first:
        in_specs = [smem, smem, whole, whole, col, col, wd_spec]
        args = (clip, lengths, x_rows, g_rows, hidden[0], hidden[1], w_down)
        out_shape, out_specs = (big, *f_out, turned, turned), (col, *f_spec, t_spec, t_spec)
    else:
        in_specs = [smem, smem, whole, whole, pl.BlockSpec((1, dim, tile), lambda j: (layer, 0, j)), wd_spec]
        args = (clip, lengths, x_rows, g_rows, w_up, w_down)
        out_shape = (big, big, *f_out, turned, turned, jax.ShapeDtypeStruct((n_rows, dim), BF16))
        out_specs = (col, col, *f_spec, t_spec, t_spec, whole)
    return pl.pallas_call(
        functools.partial(grad_kernel, first, n_samples), out_shape=out_shape, grid=(steps,), in_specs=in_specs, out_specs=out_specs,
        scratch_shapes=[pltpu.VMEM((n_samples, seq, seq), F32)] * 2, name='block_grad',
        cost_estimate=pl.CostEstimate(flops=((2 if first else 4) * dim + 3 * seq) * n_rows * ff, bytes_accessed=dim * ff * 4 + n_rows * ff * 4, transcendentals=2 * n_rows * ff),
        compiler_params=pltpu.CompilerParams(vmem_limit_bytes=60 * 1024 * 1024))(*args)


def axis_weight(axis):
    return 2 * (axis + 1) + 2 * (axis // 2)


def sums_kernel(shift, split, xt_hbm, h_hbm, a_hbm, gt_hbm, rowf, colf, r_hbm, *refs):
    late_hbm = refs[0] if split < CHUNKS else None
    (lt, slab, gpiece, clip, own, s0s, s0r, rc1, rc2, rc3, obuf,
     slab_sem, g_sem, o_sem, d_send, d_recv, sems_s, sems_r) = refs[-18:]
    me = lax.axis_index('data')
    core = me % 2
    partner = me + 1 - 2 * core

    def bit_peer(chunk, stage):
        axis = (chunk + shift + stage) % 3
        weight = axis_weight(axis)
        bit = (me // weight) % 2
        return bit, me + weight * (1 - 2 * bit)

    barrier = pltpu.get_barrier_semaphore()
    pl.semaphore_signal(barrier, inc=1, device_id=(partner,), device_id_type=MESH_ID)
    for axis in range(3):
        weight = axis_weight(axis)
        peer = me + weight * (1 - 2 * ((me // weight) % 2))
        pl.semaphore_signal(barrier, inc=1, device_id=(peer,), device_id_type=MESH_ID)

    def columns(half, chunk):
        return pl.ds(pl.multiple_of((half * PER_MAT + chunk % PER_MAT) * CW, CW), CW)

    def start_slab(half, chunk, buf):
        @pl.when(chunk < PER_MAT)
        def _():
            pltpu.make_async_copy(h_hbm.at[:, columns(half, chunk)], slab.at[buf], slab_sem.at[buf]).start()

        @pl.when(chunk >= PER_MAT)
        def _():
            pltpu.make_async_copy(a_hbm.at[:, columns(half, chunk)], slab.at[buf], slab_sem.at[buf]).start()

    def wait_slab(buf):
        pltpu.make_async_copy(h_hbm.at[:, pl.ds(0, CW)], slab.at[buf], slab_sem.at[buf]).wait()

    n_pieces = gt_hbm.shape[0] // CW
    x_copy = pltpu.make_async_copy(xt_hbm, lt.at[0], g_sem.at[1])

    def g_copy(piece):
        return pltpu.make_async_copy(gt_hbm.at[pl.ds(pl.multiple_of(piece * CW, CW), CW), :], gpiece, g_sem.at[0])

    start_slab(1 - core, 0, 0)
    x_copy.start()
    start_slab(core, 0, 2)
    pl.semaphore_wait(barrier, 4)
    x_copy.wait()

    def load_clip(chunk, buf):
        scale = jnp.where(chunk < PER_MAT, rowf[...], 1.0)
        clip[...] = (slab[buf].astype(F32) * scale).astype(BF16)

    def partner_chunk(chunk):
        buf = chunk % 2
        wait_slab(buf)
        load_clip(chunk, buf)

        @pl.when(chunk + 1 < CHUNKS)
        def _():
            start_slab(1 - core, chunk + 1, 1 - buf)

        mat = chunk // PER_MAT
        for q in range(4):
            rows = pl.ds(q * 512, 512)
            s0s[buf, rows, :] = jnp.dot(lt[mat, rows, :], clip[...], preferred_element_type=F32).astype(BF16)

    def d2d(chunk):
        buf = chunk % 2
        return pltpu.make_async_remote_copy(s0s.at[buf], s0r.at[buf], d_send.at[buf], d_recv.at[buf], device_id=(partner,), device_id_type=MESH_ID)

    def own_chunk(chunk):
        buf = 2 + chunk % 2
        wait_slab(buf)
        load_clip(chunk, buf)

        @pl.when(chunk + 1 < CHUNKS)
        def _():
            start_slab(core, chunk + 1, 5 - buf)

        d2d(chunk).wait()
        mat = chunk // PER_MAT
        for q in range(4):
            rows = pl.ds(q * 512, 512)
            part = jnp.dot(lt[mat, rows, :], clip[...], preferred_element_type=F32)
            own[chunk % OWN, rows, :] = (part + s0r[chunk % 2, rows, :].astype(F32)).astype(BF16)

    def kept_row(chunk, stage):
        row = 0
        for s in range(stage):
            bit, _ = bit_peer(chunk, s)
            row = row + bit * (1024 // (2 ** s))
        return row

    recv_bufs = (rc1, rc2, rc3)

    def stage_copy(chunk, stage):
        size = 1024 // (2 ** stage)
        bit, peer = bit_peer(chunk, stage)
        row = kept_row(chunk, stage) + (1 - bit) * size
        slot = chunk % RECV
        return pltpu.make_async_remote_copy(
            own.at[chunk % OWN, pl.ds(pl.multiple_of(row, CW), size), :], recv_bufs[stage].at[slot],
            sems_s.at[stage, slot], sems_r.at[stage, slot], device_id=(peer,), device_id_type=MESH_ID)

    def stage_sum(chunk, stage):
        size = 1024 // (2 ** stage)
        rows = pl.ds(pl.multiple_of(kept_row(chunk, stage + 1), CW), size)
        return rows, own[chunk % OWN, rows, :].astype(F32) + recv_bufs[stage][chunk % RECV].astype(F32)

    def start_out(chunk):
        @pl.when(chunk < split)
        def _():
            pltpu.make_async_copy(obuf.at[chunk % 2], r_hbm.at[chunk], o_sem.at[chunk % 2]).start()

        if split < CHUNKS:
            @pl.when(chunk >= split)
            def _():
                pltpu.make_async_copy(obuf.at[chunk % 2], late_hbm.at[chunk - split], o_sem.at[chunk % 2]).start()

    def wait_out(chunk):
        pltpu.make_async_copy(obuf.at[chunk % 2], r_hbm.at[0], o_sem.at[chunk % 2]).wait()

    partner_chunk(0)
    g_copy(0).start()
    d2d(0).start()

    def step(t, _):
        @pl.when(t >= LAG3)
        def _():
            chunk = t - LAG3
            stage_copy(chunk, 2).wait()
            _, total = stage_sum(chunk, 2)

            @pl.when(chunk >= 2)
            def _():
                wait_out(chunk - 2)

            @pl.when(chunk < PER_MAT)
            def _():
                obuf[chunk % 2] = total.astype(BF16)

            @pl.when(chunk >= PER_MAT)
            def _():
                obuf[chunk % 2] = total.T.astype(BF16)

            start_out(chunk)

        @pl.when((t >= LAG2) & (t < CHUNKS + LAG2))
        def _():
            chunk = t - LAG2
            stage_copy(chunk, 1).wait()
            rows, total = stage_sum(chunk, 1)
            own[chunk % OWN, rows, :] = total.astype(BF16)

        @pl.when((t >= LAG1) & (t < CHUNKS + LAG1))
        def _():
            chunk = t - LAG1
            stage_copy(chunk, 0).wait()
            rows, total = stage_sum(chunk, 0)
            own[chunk % OWN, rows, :] = total.astype(BF16)

        @pl.when((t >= 1) & (t < CHUNKS + 1))
        def _():
            stage_copy(t - 1, 0).start()

        @pl.when(t < n_pieces)
        def _():
            g_copy(t).wait()
            lt[1, pl.ds(pl.multiple_of(t * CW, CW), CW), :] = (gpiece[...].astype(F32) * colf[...]).astype(BF16)

            @pl.when(t + 1 < n_pieces)
            def _():
                g_copy(t + 1).start()

        @pl.when(t < CHUNKS - 1)
        def _():
            partner_chunk(t + 1)

        @pl.when(t < CHUNKS)
        def _():
            own_chunk(t)

        @pl.when(t < CHUNKS - 1)
        def _():
            d2d(t + 1).start()

        @pl.when((t >= LAG1) & (t < CHUNKS + LAG1))
        def _():
            stage_copy(t - LAG1, 1).start()

        @pl.when((t >= LAG2) & (t < CHUNKS + LAG2))
        def _():
            stage_copy(t - LAG2, 2).start()

        return 0

    lax.fori_loop(0, CHUNKS + LAG3, step, 0)
    wait_out(CHUNKS - 2)
    wait_out(CHUNKS - 1)


def block_sums(layer, split, x_turned, h_rows, a_rows, g_turned, factors):
    dim, n_rows = x_turned.shape
    scratch = [
        pltpu.VMEM((2, dim, n_rows), BF16), pltpu.VMEM((4, n_rows, CW), BF16), pltpu.VMEM((CW, n_rows), BF16), pltpu.VMEM((n_rows, CW), BF16),
        pltpu.VMEM((OWN, dim, CW), BF16), pltpu.VMEM((2, dim, CW), BF16), pltpu.VMEM((2, dim, CW), BF16),
        pltpu.VMEM((RECV, dim // 2, CW), BF16), pltpu.VMEM((RECV, dim // 4, CW), BF16), pltpu.VMEM((RECV, dim // 8, CW), BF16),
        pltpu.VMEM((2, CW, CW), BF16),
        pltpu.SemaphoreType.DMA((4,)), pltpu.SemaphoreType.DMA((2,)), pltpu.SemaphoreType.DMA((2,)),
        pltpu.SemaphoreType.DMA((2,)), pltpu.SemaphoreType.DMA((2,)), pltpu.SemaphoreType.DMA((3, RECV)), pltpu.SemaphoreType.DMA((3, RECV)),
    ]
    flops = 4 * n_rows * dim * h_rows.shape[1]
    sizes = (split, CHUNKS - split) if split < CHUNKS else (CHUNKS,)
    return pl.pallas_call(
        functools.partial(sums_kernel, 2 * layer, split),
        out_shape=tuple(jax.ShapeDtypeStruct((n, CW, CW), BF16) for n in sizes),
        in_specs=[ANY, ANY, ANY, ANY] + [pl.BlockSpec(memory_space=pltpu.VMEM)] * 2,
        out_specs=(ANY,) * len(sizes),
        scratch_shapes=scratch,
        compiler_params=pltpu.CompilerParams(collective_id=layer, has_side_effects=True, vmem_limit_bytes=60 * 1024 * 1024),
        cost_estimate=pl.CostEstimate(flops=flops, bytes_accessed=4 * n_rows * h_rows.shape[1], transcendentals=0),
        name=f'sums_{layer}',
    )(x_turned, h_rows, a_rows, g_turned, *factors)


def owner_of(chunk, piece, half, shift):
    color = (chunk + shift) % 3
    b1, b2, b3 = piece // 4, (piece // 2) % 2, piece % 2
    return b1 * axis_weight(color) + b2 * axis_weight((color + 1) % 3) + b3 * axis_weight((color + 2) % 3) + half


def finish_kernel(n_in, scale, *refs):
    pieces, noise, out = refs[:n_in], refs[n_in], refs[-1]
    across = out.shape[2] // CW
    for i in range(n_in):
        rows, cols = pl.ds(i // across * CW, CW), pl.ds(i % across * CW, CW)
        out[0, rows, cols] = (pieces[i][0, 0].astype(F32) + noise[0, rows, cols]) * scale


def finish_call(name, layer, grid, piece_specs, tile, gathered, noise, prev, batch_total):
    in_specs = piece_specs + [tile]
    args = [gathered] * len(piece_specs) + [noise]
    aliases = {}
    if prev is not None:
        in_specs.append(ANY)
        args.append(prev)
        aliases = {len(args) - 1: 0}
    steps = grid[0] * grid[1]
    size = steps * tile.block_shape[1] * tile.block_shape[2]
    return pl.pallas_call(
        functools.partial(finish_kernel, len(piece_specs), 1.0 / batch_total),
        out_shape=jax.ShapeDtypeStruct(noise.shape, F32), grid=grid, in_specs=in_specs, out_specs=tile,
        input_output_aliases=aliases, name=f'{name}_{layer}',
        cost_estimate=pl.CostEstimate(flops=size * 200, bytes_accessed=size * 10, transcendentals=0),
        compiler_params=pltpu.CompilerParams(vmem_limit_bytes=50 * 1024 * 1024))(*args)


def finish_up(layer, gathered, offset, start, n, noise, prev, batch_total):
    layers, dim, ff = noise.shape
    shift = 2 * layer

    def piece_spec(c):
        return pl.BlockSpec((1, 1, CW, CW), lambda i, k, c=c: (owner_of(start + c, i, k, shift), start - offset + c, 0, 0))

    per_half = ff // 2 // (n * CW)
    tile = pl.BlockSpec((1, CW, n * CW), lambda i, k: (layer, i, k * per_half + start // n))
    return finish_call('finish_up', layer, (dim // CW, 2), [piece_spec(c) for c in range(n)], tile, gathered, noise, prev, batch_total)


def finish_down(layer, gathered, offset, start, n, noise, prev, batch_total):
    layers, ff, dim = noise.shape
    shift, n_in = 2 * layer, dim // CW

    def piece_spec(d, i):
        def index(k, c):
            chunk = start + 2 * c + d
            return owner_of(chunk, i, k, shift), chunk - offset, 0, 0

        return pl.BlockSpec((1, 1, CW, CW), index)

    tile = pl.BlockSpec((1, 2 * CW, dim), lambda k, c: (layer, (k * PER_MAT + start - PER_MAT) // 2 + c, 0))
    specs = [piece_spec(d, i) for d in range(2) for i in range(n_in)]
    return finish_call('finish_down', layer, (2, n // 2), specs, tile, gathered, noise, prev, batch_total)


def per_device(x_in, dy_out, lengths, w_up, w_down, noise_up, noise_down, clip_norm, batch_total):
    n_samples, seq_len, dim = x_in.shape
    n_rows = n_samples * seq_len
    x_first = x_in.reshape(n_rows, dim)
    z_first, a_first, x_last = forward_block(0, x_first, w_up, w_down)
    a_last, h_last, row_f, col_f, x_turned, g_turned, g_last = block_grad(1, x_last, dy_out.reshape(n_rows, dim), None, w_up, w_down, clip_norm[1:], lengths)
    piece, = block_sums(1, CHUNKS, x_turned, h_last, a_last, g_turned, (row_f, col_f))
    gathered_last = lax.all_gather(piece, 'data')
    g_first = add_product(1, g_last, h_last, w_up, True)
    h_first, row_f, col_f, x_turned, g_turned = block_grad(0, x_first, g_first, (z_first, a_first), w_up, w_down, clip_norm[:1], lengths)
    pieces = block_sums(0, SPLIT, x_turned, h_first, a_first, g_turned, (row_f, col_f))
    part_a, part_b = [lax.all_gather(part, 'data') for part in pieces]
    grad_up = finish_up(1, gathered_last, 0, 0, PER_MAT, noise_up, None, batch_total)
    grad_down = finish_down(1, gathered_last, 0, PER_MAT, PER_MAT, noise_down, None, batch_total)
    grad_up, grad_down, part_a = lax.optimization_barrier((grad_up, grad_down, part_a))
    grad_up = finish_up(0, part_a, 0, 0, PER_MAT, noise_up, grad_up, batch_total)
    grad_down = finish_down(0, part_a, 0, PER_MAT, SPLIT - PER_MAT, noise_down, grad_down, batch_total)
    grad_up, grad_down, part_b = lax.optimization_barrier((grad_up, grad_down, part_b))
    grad_down = finish_down(0, part_b, SPLIT, SPLIT, CHUNKS - SPLIT, noise_down, grad_down, batch_total)
    return grad_up, grad_down


def solution(mesh):
    batch_spec = P('data', None, None)

    def grad_step(x_in, dy_out, lengths, w_up, w_down, noise_up, noise_down, clip_norm):
        device_fn = functools.partial(per_device, batch_total=x_in.shape[0])
        mapped = jax.shard_map(device_fn, mesh=mesh, in_specs=(batch_spec, batch_spec, P('data'), P(), P(), P(), P(), P()), out_specs=(P(), P()), check_vma=False)
        return mapped(x_in, dy_out, lengths, w_up, w_down, noise_up, noise_down, clip_norm)

    return grad_step
```

time: 1360 us -> 1280 us (0.941)
  waiting for transfers between devices: 126 us -> 78.1 us
  Pallas kernels: 1200 us -> 1180 us
    pallas_call x2 -> x1, Pallas kernels: 124 us -> 62 us  [add_product(): pl.pallas_call(functools.partial(add_kernel, transposed), out_shape=jax.S...]
    all_gather x2 -> x3, waiting for transfers between devices: 126 us -> 77.3 us  [the longest x2 77.3 us: per_device(): part_a, part_b = [lax.all_gather(part, 'data') for part in pieces]]
    pallas_call x9 -> x10, Pallas kernels: 1080 us -> 1120 us  [the longest x2 529 us: block_sums(): pl.pallas_call(functools.partial(sums_kernel, 2 * layer, split), out_shap...]
  transfers between devices with their start and end apart: 2 -> 3, of which waited for: 1 -> 1; matrix products, arithmetic and copies ran while one was open for 0% -> 0% of each run, Pallas kernels for 42% -> 50%
where the time goes in v2:
time: 1280 us
  Pallas kernels  1180 us (92%)
  waiting for transfers between devices  78.1 us (6%)
  between operations  14.1 us (1%)
    pallas_call x2, Pallas kernels, block_sums(): pl.pallas_call(functools.partial(sums_kernel, 2 * layer, split), out_shap...  529 us
    pallas_call x2, Pallas kernels, block_grad(): pl.pallas_call(functools.partial(grad_kernel, first, n_samples), out_shap...  251 us
    pallas_call x5, Pallas kernels, finish_call(): pl.pallas_call(functools.partial(finish_kernel, len(piece_specs), 1.0 / b...  216 us
    pallas_call x1, Pallas kernels, forward_block(): pl.pallas_call(functools.partial(forward_kernel, n_rows // 2), out_shape=...  123 us
    all_gather x2, waiting for transfers between devices, per_device(): part_a, part_b = [lax.all_gather(part, 'data') for part in pieces]  77.3 us
    pallas_call x1, Pallas kernels, add_product(): pl.pallas_call(functools.partial(add_kernel, transposed), out_shape=jax.S...  62 us
  transfers between devices with their start and end apart: 3, of which 1 were waited for; matrix products, arithmetic and copies ran while one was open for 0% of the time, Pallas kernels for 50%

profile of v2, /device:TPU:0, one launch (start us, length us, event | category | flops | bytes accessed | tf_op | source)
XLA Modules:
  0.0 1275.3 jit_solution(15746385312357473716)
XLA Ops:
  7.2 0.0 all-gather.7.cloned.1.call-start
  7.2 1.4 fusion
  8.6 123.2 %forward_block.1 = (bf16[1536,8192]{1,0:T(8,128)(2,1)}, bf16[1536,8192]{1,0:T(8,128)(2,1)}, bf16[1536,2048]{1,0:T(8,128)(2,1)}) custom-call(bf16[1536,2048]{1,0:T(8,128)(2,1)} %bitcast.54, bf16[2,2048,8192]{2,1,0:T(8,128)(2,1)} %w_ref.1, bf16[2,8192,2048]{2,1,0:T(8,128)(2,1)} %refs_2_.1), custom_call_target="tpu_custom_call" | custom-call | flops 103079215104 | bytes 117440512 | tf_op jit(solution)/shard_map/forward_block/pallas_call | solution.py:61
  131.8 150.9 %block_grad.2 = (bf16[1536,8192]{1,0:T(8,128)(2,1)}, bf16[1536,8192]{1,0:T(8,128)(2,1)}, f32[1536,1]{1,0:T(8,128)}, f32[1,1536]{1,0:T(1,128)}, bf16[2048,1536]{1...) custom-call(f32[1]{0:T(128)} %get-tuple-element.49.clip_ref, s32[3]{0:T(128)} %len_ref.3, ...), custom_call_target="tpu_custom_call" | custom-call | flops 122406567936 | bytes 117440512 | tf_op jit(solution)/shard_map/block_grad/pallas_call | solution.py:193
  282.6 239.0 %sums_1.1 = bf16[32,256,256]{2,1,0:T(8,128)(2,1)} custom-call(bf16[2048,1536]{1,0:T(8,128)(2,1)} %get-tuple-element.26.xt_hbm, bf16[1536,8192]{1,0:T(8,128)(2,1)} %get-tuple-element.27.h_hbm.a_ref, bf16[1536,8192]{1,0:T(8,128)(2,1)} %get-tuple-element.28.a_hbm, bf16[2048,1536]{1,0:T(8,128)(2,1)} %get-tuple-element.29.gt_hbm, ...), custom_call_target="tpu_custom_call" | custom-call | flops 103079215104 | bytes 50331648 | tf_op jit(solution)/shard_map/sums_1/pallas_call | solution.py:417
  521.6 0.0 all-gather.7.cloned.1.call-update
  521.6 0.0 all-gather.9.cloned.1.call-start
  521.7 62.0 %add_product.1.g_in = bf16[1536,2048]{1,0:T(8,128)(2,1)} custom-call(bf16[1536,8192]{1,0:T(8,128)(2,1)} %get-tuple-element.27.h_hbm.a_ref, bf16[2,2048,8192]{2,1,0:T(8,128)(2,1)} %w_ref.1, bf16[1536,2048]{1,0:T(8,128)(2,1)} %get-tuple-element.32.x_ref), custom_call_target="tpu_custom_call" | custom-call | flops 51539607552 | bytes 83886080 | tf_op jit(solution)/shard_map/add_product/pallas_call | solution.py:97
  583.7 100.0 %block_grad.3 = (bf16[1536,8192]{1,0:T(8,128)(2,1)}, f32[1536,1]{1,0:T(8,128)}, f32[1,1536]{1,0:T(1,128)}, bf16[2048,1536]{1,0:T(8,128)(2,1)}, bf16[2048,1536]{1,0:T(8,128)(2,1)}) custom-call(f32[1]{0:T(128)} %get-tuple-element.48.clip_ref, s32[3]{0:T(128)} %len_ref.3, bf16[1536,2048]{1,0:T(8,128)(2,1)} %bitcast.55, bf16[1536,2048]{1,0:T(8,128)(2,1)} %add_product.1.g_in, ...), custom_call_target="tpu_custom_call" | custom-call | flops 70866960384 | bytes 117440512 | tf_op jit(solution)/shard_map/block_grad/pallas_call | solution.py:193
  683.7 290.5 %sums_0.1 = (bf16[24,256,256]{2,1,0:T(8,128)(2,1)}, bf16[8,256,256]{2,1,0:T(8,128)(2,1)}) custom-call(bf16[2048,1536]{1,0:T(8,128)(2,1)} %get-tuple-element.35.xt_hbm, bf16[1536,8192]{1,0:T(8,128)(2,1)} %get-tuple-element.36.h_hbm, bf16[1536,8192]{1,0:T(8,128)(2,1)} %get-tuple-element.34.refs_1_.a_hbm, bf16[2048,1536]{1,0:T(8,128)(2,1)} %get-tuple-element.37.gt_hbm, ...), custom_call_target="tpu_custom_call" | custom-call | flops 103079215104 | bytes 50331648 | tf_op jit(solution)/shard_map/sums_0/pallas_call | solution.py:417
  974.2 0.0 all-gather.9.cloned.1.call-update
  974.3 0.0 all-gather.11.cloned.1.call-start
  974.3 0.7 all-gather.11.cloned.1.call-update
  975.0 0.0 all-gather.7.cloned.1.call-done
  975.0 53.8 %finish_up_1.1.refs_17_ = f32[2,2048,8192]{2,1,0:T(8,128)} custom-call(bf16[16,32,256,256]{3,2,1,0:T(8,128)(2,1)} %bitcast.2.refs_0_.refs_1_.refs_2_.refs_3_.refs_4_.refs_5_.refs_6_.refs_7_.refs_8_.refs_9_.refs_10_.refs_11_.refs_12_.refs_13_.refs_14_.refs_15_, ...), custom_call_target="tpu_custom_call" | custom-call | flops 3355443200 | bytes 167772160 | tf_op jit(solution)/shard_map/finish_up_1/pallas_call | solution.py:453
  1028.9 53.5 %finish_down_1.1.refs_17_ = f32[2,8192,2048]{2,1,0:T(8,128)} custom-call(bf16[16,32,256,256]{3,2,1,0:T(8,128)(2,1)} %bitcast.2.refs_0_.refs_1_.refs_2_.refs_3_.refs_4_.refs_5_.refs_6_.refs_7_.refs_8_.refs_9_.refs_10_.refs_11_.refs_12_.refs_13_.refs_14_.refs_15_, ...), custom_call_target="tpu_custom_call" | custom-call | flops 3355443200 | bytes 167772160 | tf_op jit(solution)/shard_map/finish_down_1/pallas_call | solution.py:453
  1082.3 77.3 %all-gather.9.cloned.1.call-done = bf16[384,256,256]{2,1,0:T(8,128)(2,1)} async-done(((bf16[24,256,256]{2,1,0:T(8,128)(2,1)}), bf16[384,256,256]{2,1,0:T(8,128)(2,1)}) %all-gather.9.cloned.1.call-update) | async-done | bytes 50331664 | tf_op jit(solution)/shard_map/all_gather | solution.py:500
  1159.6 27.5 %finish_down_0.2.refs_17_ = f32[2,8192,2048]{2,1,0:T(8,128)} custom-call(bf16[16,24,256,256]{3,2,1,0:T(8,128)(2,1)} %bitcast.20, bf16[16,24,256,256]{3,2,1,0:T(8,128)(2,1)} %bitcast.6, bf16[16,24,256,256]{3,2,1,0:T(8,128)(2,1)} %bitcast.7, bf16[16,24,256,256]{3,2,1,0:T(8,128)(2,1)} %bitcast.8, ...), custom_call_target="tpu_custom_call", output_to_operand_aliasing={{}: (17, {})} | custom-call | flops 1677721600 | bytes 83886080 | tf_op jit(solution)/shard_map/finish_down_0/pallas_call | solution.py:453
  1187.1 53.9 %finish_up_0.1 = f32[2,2048,8192]{2,1,0:T(8,128)} custom-call(bf16[16,24,256,256]{3,2,1,0:T(8,128)(2,1)} %bitcast.21, bf16[16,24,256,256]{3,2,1,0:T(8,128)(2,1)} %bitcast.22, bf16[16,24,256,256]{3,2,1,0:T(8,128)(2,1)} %bitcast.23, bf16[16,24,256,256]{3,2,1,0:T(8,128)(2,1)} %bitcast.24, ...), custom_call_target="tpu_custom_call", output_to_operand_aliasing={{}: (17, {})} | custom-call | flops 3355443200 | bytes 167772160 | tf_op jit(solution)/shard_map/finish_up_0/pallas_call | solution.py:453
  1241.0 0.0 all-gather.11.cloned.1.call-done
  1241.0 27.5 %finish_down_0.3 = f32[2,8192,2048]{2,1,0:T(8,128)} custom-call(bf16[16,8,256,256]{3,2,1,0:T(8,128)(2,1)} %bitcast.37, bf16[16,8,256,256]{3,2,1,0:T(8,128)(2,1)} %bitcast.38, bf16[16,8,256,256]{3,2,1,0:T(8,128)(2,1)} %bitcast.39, bf16[16,8,256,256]{3,2,1,0:T(8,128)(2,1)} %bitcast.40, ...), custom_call_target="tpu_custom_call", output_to_operand_aliasing={{}: (17, {})} | custom-call | flops 1677721600 | bytes 83886080 | tf_op jit(solution)/shard_map/finish_down_0/pallas_call | solution.py:453
Async XLA Ops:
  7.2 967.9 %all-gather.7.cloned.1.call-start = ((), (), s32[]{:S(2)}) async-start(), calls=%async_computation | async-start | bytes 71303168 | tf_op jit(solution)/shard_map/all_gather | solution.py:496
  521.6 638.0 %all-gather.9.cloned.1.call-start = ((), (), s32[]{:S(2)}) async-start(), calls=%async_computation.1 | async-start | bytes 53477376 | tf_op jit(solution)/shard_map/all_gather | solution.py:500
  974.3 266.7 %all-gather.11.cloned.1.call-start = ((), (), s32[]{:S(2)}) async-start(), calls=%async_computation.2 | async-start | bytes 17825792 | tf_op jit(solution)/shard_map/all_gather | solution.py:500
Sparse Core Ops, SparseCore 0:
  521.8 298.0 all-gather.6
  974.4 185.2 all-gather.8
  1161.9 76.0 all-gather.10

commit v3 on v2

--- a/solution.py
+++ b/solution.py
@@ -27,43 +27,126 @@
     return lax.dot_general(a, b, (((1,), (1,)), ((), ())), preferred_element_type=F32)
 
 
-def forward_kernel(block, x_ref, wu_ref, wd_ref, z_ref, a_ref, o_ref, acc):
-    j = pl.program_id(0)
-
-    @pl.when(j == 0)
-    def _():
-        acc[...] = x_ref[...].astype(F32)
-
-    for start in range(0, x_ref.shape[0], block):
-        rows = pl.ds(start, block)
-        z = jnp.dot(x_ref[rows, :], wu_ref[0], preferred_element_type=F32).astype(BF16)
-        z_ref[rows, :] = z
-        zf = z.astype(F32)
-        a = (zf * normal_cdf(zf)).astype(BF16)
-        a_ref[rows, :] = a
-        acc[rows, :] += jnp.dot(a, wd_ref[0], preferred_element_type=F32)
-
-    @pl.when(j == pl.num_programs(0) - 1)
-    def _():
-        o_ref[...] = acc[...].astype(BF16)
-
-
 def resident(shape):
     return pl.BlockSpec(shape, lambda j: (0, 0), pipeline_mode=pl.Buffered(buffer_count=1))
 
 
-def forward_block(layer, x_rows, w_up, w_down):
+def add_grams(gram, s, block):
+    half = block.shape[0] // 2
+    low, high = slice(0, half), slice(half, 2 * half)
+    gram[s, low, low] += dot_nt(block[low], block[low])
+    gram[s, high, :] += dot_nt(block[high], block)
+
+
+def write_factors(n_samples, clip, x_ref, g_ref, gram_a, gram_h, fr_ref, f_ref):
+    seq = x_ref.shape[0] // n_samples
+    half = seq // 2
+    low, high = slice(0, half), slice(half, seq)
+    for s in range(n_samples):
+        first_half, second_half = pl.ds(s * seq, half), pl.ds(s * seq + half, half)
+
+        def paired(r, rr, c, cc):
+            gg = dot_nt(g_ref[rr, :], g_ref[cc, :])
+            xx = dot_nt(x_ref[rr, :], x_ref[cc, :])
+            return gram_a[s, r, c] * gg + gram_h[s, r, c] * xx
+
+        total = (paired(low, first_half, low, first_half) + paired(high, second_half, high, second_half)
+                 + 2.0 * paired(high, second_half, low, first_half))
+        norm_sq = jnp.sum(total, axis=(0, 1), keepdims=True)
+        factor = jnp.minimum(1.0, clip / jnp.sqrt(norm_sq))
+        f_ref[:, pl.ds(s * seq, seq)] = jnp.broadcast_to(factor, (1, seq))
+        fr_ref[pl.ds(s * seq, seq), :] = jnp.broadcast_to(factor, (seq, 1))
+
+
+def turn_columns(j, x_ref, g_ref, xt_ref, gt_ref):
+    width = xt_ref.shape[0]
+    cols = pl.ds(pl.multiple_of(j * width, width), width)
+    xt_ref[...] = x_ref[:, cols].T
+    gt_ref[...] = g_ref[:, cols].T
+
+
+def gelu_slope(z, cdf):
+    return cdf + z * jnp.exp(-0.5 * z * z) * 0.3989422804014327
+
+
+def first_kernel(n_samples, steps, clip_ref, len_ref, x_hbm, dy_hbm, wu_ref, wd_ref, z_ref, a_first, a_ref, h_ref, fr_ref, f_ref, xt_ref, gt_ref, g_ref,
+                 x_ref, acc, gram_a, gram_h, sems):
+    j = pl.program_id(0)
+    n_rows = x_ref.shape[0]
+    seq = n_rows // n_samples
+    x_copy = pltpu.make_async_copy(x_hbm, x_ref, sems.at[0])
+    g_copy = pltpu.make_async_copy(dy_hbm, g_ref, sems.at[1])
+
+    @pl.when(j == 0)
+    def _():
+        x_copy.start()
+        g_copy.start()
+        x_copy.wait()
+        acc[...] = x_ref[...].astype(F32)
+
+    @pl.when(j < steps)
+    def _():
+        block = n_rows // 2
+        for start in range(0, n_rows, block):
+            rows = pl.ds(start, block)
+            z = jnp.dot(x_ref[rows, :], wu_ref[0], preferred_element_type=F32).astype(BF16)
+            z_ref[rows, :] = z
+            zf = z.astype(F32)
+            a = (zf * normal_cdf(zf)).astype(BF16)
+            a_first[rows, :] = a
+            acc[rows, :] += jnp.dot(a, wd_ref[0], preferred_element_type=F32)
+
+    @pl.when(j == steps)
+    def _():
+        x_ref[...] = acc[...].astype(BF16)
+        gram_a[...] = jnp.zeros_like(gram_a)
+        gram_h[...] = jnp.zeros_like(gram_h)
+        g_copy.wait()
+        for s in range(n_samples):
+            rows = pl.ds(s * seq, seq)
+            valid = lax.broadcasted_iota(jnp.int32, (seq, 1), 0) < len_ref[s]
+            g_ref[rows, :] = jnp.where(valid, g_ref[rows, :].astype(F32), 0.0).astype(BF16)
+
+    @pl.when(j >= steps)
+    def _():
+        turn_columns(j - steps, x_ref, g_ref, xt_ref, gt_ref)
+        for s in range(n_samples):
+            rows = pl.ds(s * seq, seq)
+            z = jnp.dot(x_ref[rows, :], wu_ref[0], preferred_element_type=F32).astype(BF16).astype(F32)
+            u = dot_nt(g_ref[rows, :], wd_ref[0])
+            cdf = normal_cdf(z)
+            a = (z * cdf).astype(BF16)
+            a_ref[rows, :] = a
+            h = (u * gelu_slope(z, cdf)).astype(BF16)
+            h_ref[rows, :] = h
+            add_grams(gram_a, s, a)
+            add_grams(gram_h, s, h)
+
+    @pl.when(j == 2 * steps - 1)
+    def _():
+        write_factors(n_samples, clip_ref[1], x_ref, g_ref, gram_a, gram_h, fr_ref, f_ref)
+
+
+def first_pass(x_rows, dy_rows, w_up, w_down, clip_norm, lengths):
     n_rows, dim = x_rows.shape
+    n_samples = lengths.shape[0]
     ff = w_up.shape[2]
     tile = 512
+    steps = ff // tile
+    seq = n_rows // n_samples
+    early = pl.BlockSpec((n_rows, tile), lambda j: (0, jnp.minimum(j, steps - 1)))
+    late = pl.BlockSpec((n_rows, tile), lambda j: (0, jnp.maximum(j - steps, 0)))
+    turned, t_spec = jax.ShapeDtypeStruct((dim, n_rows), BF16), pl.BlockSpec((dim // steps, n_rows), lambda j: (jnp.maximum(j - steps, 0), 0))
     big = jax.ShapeDtypeStruct((n_rows, ff), BF16)
-    col = pl.BlockSpec((n_rows, tile), lambda j: (0, j))
+    smem = pl.BlockSpec(memory_space=pltpu.SMEM)
     return pl.pallas_call(
-        functools.partial(forward_kernel, n_rows // 2), out_shape=(big, big, jax.ShapeDtypeStruct((n_rows, dim), BF16)), grid=(ff // tile,),
-        in_specs=[resident((n_rows, dim)), pl.BlockSpec((1, dim, tile), lambda j: (layer, 0, j)), pl.BlockSpec((1, tile, dim), lambda j: (layer, j, 0))],
-        out_specs=(col, col, resident((n_rows, dim))), scratch_shapes=[pltpu.VMEM((n_rows, dim), F32)], name='forward_block',
-        cost_estimate=pl.CostEstimate(flops=4 * n_rows * dim * ff, bytes_accessed=dim * ff * 4 + n_rows * ff * 4, transcendentals=n_rows * ff),
-        compiler_params=pltpu.CompilerParams(vmem_limit_bytes=63 * 1024 * 1024))(x_rows, w_up, w_down)
+        functools.partial(first_kernel, n_samples, steps), grid=(2 * steps,), name='first_pass',
+        out_shape=(big, big, big, big, jax.ShapeDtypeStruct((n_rows, 1), F32), jax.ShapeDtypeStruct((1, n_rows), F32), turned, turned, jax.ShapeDtypeStruct((n_rows, dim), BF16)),
+        in_specs=[smem, smem, ANY, ANY, pl.BlockSpec((1, dim, tile), lambda j: (j // steps, 0, j % steps)), pl.BlockSpec((1, tile, dim), lambda j: (j // steps, j % steps, 0))],
+        out_specs=(early, early, late, late, resident((n_rows, 1)), resident((1, n_rows)), t_spec, t_spec, resident((n_rows, dim))),
+        scratch_shapes=[pltpu.VMEM((n_rows, dim), BF16), pltpu.VMEM((n_rows, dim), F32)] + [pltpu.VMEM((n_samples, seq, seq), F32)] * 2 + [pltpu.SemaphoreType.DMA((2,))],
+        cost_estimate=pl.CostEstimate(flops=(8 * dim + 3 * seq) * n_rows * ff, bytes_accessed=dim * ff * 8 + n_rows * ff * 8, transcendentals=3 * n_rows * ff),
+        compiler_params=pltpu.CompilerParams(vmem_limit_bytes=63 * 1024 * 1024))(clip_norm, lengths, x_rows, dy_rows, w_up, w_down)
 
 
 def add_kernel(transposed, a_ref, w_ref, x_ref, o_ref, acc):
@@ -102,99 +185,47 @@
         compiler_params=pltpu.CompilerParams(vmem_limit_bytes=60 * 1024 * 1024))(a_rows, weight, x_rows)
 
 
-def grad_kernel(first, n_samples, clip_ref, len_ref, x_ref, g_in, *refs):
-    if first:
-        g_ref = g_in
-        z_ref, a_ref, wd_ref, h_ref, fr_ref, f_ref, xt_ref, gt_ref, gram_a, gram_h = refs
-    else:
-        wu_ref, wd_ref, a_ref, h_ref, fr_ref, f_ref, xt_ref, gt_ref, g_ref, gram_a, gram_h = refs
+def grad_kernel(n_samples, clip_ref, x_ref, g_ref, z_ref, a_ref, wd_ref, h_ref, fr_ref, f_ref, xt_ref, gt_ref, gram_a, gram_h):
     j = pl.program_id(0)
     seq = x_ref.shape[0] // n_samples
-    half = seq // 2
-    low, high = slice(0, half), slice(half, seq)
 
     @pl.when(j == 0)
     def _():
         gram_a[...] = jnp.zeros_like(gram_a)
         gram_h[...] = jnp.zeros_like(gram_h)
-        if not first:
-            for s in range(n_samples):
-                rows = pl.ds(s * seq, seq)
-                valid = lax.broadcasted_iota(jnp.int32, (seq, 1), 0) < len_ref[s]
-                g_ref[rows, :] = jnp.where(valid, g_in[rows, :].astype(F32), 0.0).astype(BF16)
-
-    width = xt_ref.shape[0]
-    cols = pl.ds(pl.multiple_of(j * width, width), width)
-    xt_ref[...] = x_ref[:, cols].T
-    gt_ref[...] = g_ref[:, cols].T
+
+    turn_columns(j, x_ref, g_ref, xt_ref, gt_ref)
     for s in range(n_samples):
         rows = pl.ds(s * seq, seq)
-        if first:
-            z = z_ref[rows, :].astype(F32)
-        else:
-            z = jnp.dot(x_ref[rows, :], wu_ref[0], preferred_element_type=F32).astype(BF16).astype(F32)
+        z = z_ref[rows, :].astype(F32)
         u = dot_nt(g_ref[rows, :], wd_ref[0])
-        cdf = normal_cdf(z)
-        if first:
-            a = a_ref[rows, :]
-        else:
-            a = (z * cdf).astype(BF16)
-            a_ref[rows, :] = a
-        h = (u * (cdf + z * jnp.exp(-0.5 * z * z) * 0.3989422804014327)).astype(BF16)
+        h = (u * gelu_slope(z, normal_cdf(z))).astype(BF16)
         h_ref[rows, :] = h
-        gram_a[s, low, low] += dot_nt(a[low], a[low])
-        gram_a[s, high, :] += dot_nt(a[high], a)
-        gram_h[s, low, low] += dot_nt(h[low], h[low])
-        gram_h[s, high, :] += dot_nt(h[high], h)
+        add_grams(gram_a, s, a_ref[rows, :])
+        add_grams(gram_h, s, h)
 
     @pl.when(j == pl.num_programs(0) - 1)
     def _():
-        for s in range(n_samples):
-            first_half, second_half = pl.ds(s * seq, half), pl.ds(s * seq + half, half)
-
-            def paired(r, rr, c, cc):
-                gg = dot_nt(g_ref[rr, :], g_ref[cc, :])
-                xx = dot_nt(x_ref[rr, :], x_ref[cc, :])
-                return gram_a[s, r, c] * gg + gram_h[s, r, c] * xx
-
-            total = (paired(low, first_half, low, first_half) + paired(high, second_half, high, second_half)
-                     + 2.0 * paired(high, second_half, low, first_half))
-            norm_sq = jnp.sum(total, axis=(0, 1), keepdims=True)
-            factor = jnp.minimum(1.0, clip_ref[0] / jnp.sqrt(norm_sq))
-            f_ref[:, pl.ds(s * seq, seq)] = jnp.broadcast_to(factor, (1, seq))
-            fr_ref[pl.ds(s * seq, seq), :] = jnp.broadcast_to(factor, (seq, 1))
-
-
-def block_grad(layer, x_rows, g_rows, hidden, w_up, w_down, clip, lengths):
+        write_factors(n_samples, clip_ref[0], x_ref, g_ref, gram_a, gram_h, fr_ref, f_ref)
+
+
+def block_grad(x_rows, g_rows, z_rows, a_rows, w_down, clip_norm, n_samples):
     n_rows, dim = x_rows.shape
-    n_samples = lengths.shape[0]
-    ff = w_up.shape[2]
+    ff = z_rows.shape[1]
     tile = 512
     steps = ff // tile
     seq = n_rows // n_samples
     col = pl.BlockSpec((n_rows, tile), lambda j: (0, j))
     whole = resident((n_rows, dim))
-    wd_spec = pl.BlockSpec((1, tile, dim), lambda j: (layer, j, 0))
-    big = jax.ShapeDtypeStruct((n_rows, ff), BF16)
-    f_out = (jax.ShapeDtypeStruct((n_rows, 1), F32), jax.ShapeDtypeStruct((1, n_rows), F32))
-    f_spec = (resident((n_rows, 1)), resident((1, n_rows)))
     turned, t_spec = jax.ShapeDtypeStruct((dim, n_rows), BF16), pl.BlockSpec((dim // steps, n_rows), lambda j: (j, 0))
-    smem = pl.BlockSpec(memory_space=pltpu.SMEM)
-    first = hidden is not None
-    if first:
-        in_specs = [smem, smem, whole, whole, col, col, wd_spec]
-        args = (clip, lengths, x_rows, g_rows, hidden[0], hidden[1], w_down)
-        out_shape, out_specs = (big, *f_out, turned, turned), (col, *f_spec, t_spec, t_spec)
-    else:
-        in_specs = [smem, smem, whole, whole, pl.BlockSpec((1, dim, tile), lambda j: (layer, 0, j)), wd_spec]
-        args = (clip, lengths, x_rows, g_rows, w_up, w_down)
-        out_shape = (big, big, *f_out, turned, turned, jax.ShapeDtypeStruct((n_rows, dim), BF16))
-        out_specs = (col, col, *f_spec, t_spec, t_spec, whole)
     return pl.pallas_call(
-        functools.partial(grad_kernel, first, n_samples), out_shape=out_shape, grid=(steps,), in_specs=in_specs, out_specs=out_specs,
-        scratch_shapes=[pltpu.VMEM((n_samples, seq, seq), F32)] * 2, name='block_grad',
-        cost_estimate=pl.CostEstimate(flops=((2 if first else 4) * dim + 3 * seq) * n_rows * ff, bytes_accessed=dim * ff * 4 + n_rows * ff * 4, transcendentals=2 * n_rows * ff),
-        compiler_params=pltpu.CompilerParams(vmem_limit_bytes=60 * 1024 * 1024))(*args)
+        functools.partial(grad_kernel, n_samples), grid=(steps,), name='block_grad',
+        out_shape=(jax.ShapeDtypeStruct((n_rows, ff), BF16), jax.ShapeDtypeStruct((n_rows, 1), F32), jax.ShapeDtypeStruct((1, n_rows), F32), turned, turned),
+        in_specs=[pl.BlockSpec(memory_space=pltpu.SMEM), whole, whole, col, col, pl.BlockSpec((1, tile, dim), lambda j: (0, j, 0))],
+        out_specs=(col, resident((n_rows, 1)), resident((1, n_rows)), t_spec, t_spec),
+        scratch_shapes=[pltpu.VMEM((n_samples, seq, seq), F32)] * 2,
+        cost_estimate=pl.CostEstimate(flops=(2 * dim + 3 * seq) * n_rows * ff, bytes_accessed=dim * ff * 2 + n_rows * ff * 6, transcendentals=2 * n_rows * ff),
+        compiler_params=pltpu.CompilerParams(vmem_limit_bytes=60 * 1024 * 1024))(clip_norm, x_rows, g_rows, z_rows, a_rows, w_down)
 
 
 def axis_weight(axis):
@@ -238,22 +269,24 @@
         pltpu.make_async_copy(h_hbm.at[:, pl.ds(0, CW)], slab.at[buf], slab_sem.at[buf]).wait()
 
     n_pieces = gt_hbm.shape[0] // CW
-    x_copy = pltpu.make_async_copy(xt_hbm, lt.at[0], g_sem.at[1])
+
+    def x_copy(q):
+        rows = pl.ds(q * 512, 512)
+        return pltpu.make_async_copy(xt_hbm.at[rows, :], lt.at[0, rows, :], g_sem.at[1 + q])
 
     def g_copy(piece):
         return pltpu.make_async_copy(gt_hbm.at[pl.ds(pl.multiple_of(piece * CW, CW), CW), :], gpiece, g_sem.at[0])
 
     start_slab(1 - core, 0, 0)
-    x_copy.start()
+    for q in range(4):
+        x_copy(q).start()
     start_slab(core, 0, 2)
-    pl.semaphore_wait(barrier, 4)
-    x_copy.wait()
 
     def load_clip(chunk, buf):
         scale = jnp.where(chunk < PER_MAT, rowf[...], 1.0)
         clip[...] = (slab[buf].astype(F32) * scale).astype(BF16)
 
-    def partner_chunk(chunk):
+    def partner_chunk(chunk, opening=False):
         buf = chunk % 2
         wait_slab(buf)
         load_clip(chunk, buf)
@@ -265,6 +298,8 @@
         mat = chunk // PER_MAT
         for q in range(4):
             rows = pl.ds(q * 512, 512)
+            if opening:
+                x_copy(q).wait()
             s0s[buf, rows, :] = jnp.dot(lt[mat, rows, :], clip[...], preferred_element_type=F32).astype(BF16)
 
     def d2d(chunk):
@@ -323,8 +358,9 @@
     def wait_out(chunk):
         pltpu.make_async_copy(obuf.at[chunk % 2], r_hbm.at[0], o_sem.at[chunk % 2]).wait()
 
-    partner_chunk(0)
+    partner_chunk(0, True)
     g_copy(0).start()
+    pl.semaphore_wait(barrier, 4)
     d2d(0).start()
 
     def step(t, _):
@@ -409,7 +445,7 @@
         pltpu.VMEM((OWN, dim, CW), BF16), pltpu.VMEM((2, dim, CW), BF16), pltpu.VMEM((2, dim, CW), BF16),
         pltpu.VMEM((RECV, dim // 2, CW), BF16), pltpu.VMEM((RECV, dim // 4, CW), BF16), pltpu.VMEM((RECV, dim // 8, CW), BF16),
         pltpu.VMEM((2, CW, CW), BF16),
-        pltpu.SemaphoreType.DMA((4,)), pltpu.SemaphoreType.DMA((2,)), pltpu.SemaphoreType.DMA((2,)),
+        pltpu.SemaphoreType.DMA((4,)), pltpu.SemaphoreType.DMA((5,)), pltpu.SemaphoreType.DMA((2,)),
         pltpu.SemaphoreType.DMA((2,)), pltpu.SemaphoreType.DMA((2,)), pltpu.SemaphoreType.DMA((3, RECV)), pltpu.SemaphoreType.DMA((3, RECV)),
     ]
     flops = 4 * n_rows * dim * h_rows.shape[1]
@@ -490,12 +526,11 @@
     n_samples, seq_len, dim = x_in.shape
     n_rows = n_samples * seq_len
     x_first = x_in.reshape(n_rows, dim)
-    z_first, a_first, x_last = forward_block(0, x_first, w_up, w_down)
-    a_last, h_last, row_f, col_f, x_turned, g_turned, g_last = block_grad(1, x_last, dy_out.reshape(n_rows, dim), None, w_up, w_down, clip_norm[1:], lengths)
+    z_first, a_first, a_last, h_last, row_f, col_f, x_turned, g_turned, g_last = first_pass(x_first, dy_out.reshape(n_rows, dim), w_up, w_down, clip_norm, lengths)
     piece, = block_sums(1, CHUNKS, x_turned, h_last, a_last, g_turned, (row_f, col_f))
     gathered_last = lax.all_gather(piece, 'data')
     g_first = add_product(1, g_last, h_last, w_up, True)
-    h_first, row_f, col_f, x_turned, g_turned = block_grad(0, x_first, g_first, (z_first, a_first), w_up, w_down, clip_norm[:1], lengths)
+    h_first, row_f, col_f, x_turned, g_turned = block_grad(x_first, g_first, z_first, a_first, w_down, clip_norm, n_samples)
     pieces = block_sums(0, SPLIT, x_turned, h_first, a_first, g_turned, (row_f, col_f))
     part_a, part_b = [lax.all_gather(part, 'data') for part in pieces]
     grad_up = finish_up(1, gathered_last, 0, 0, PER_MAT, noise_up, None, batch_total)

time: 1280 us -> 1270 us (level)
    pallas_call x3 -> x2, Pallas kernels: 374 us -> 368 us  [the longest x1 268 us: first_pass(): pl.pallas_call(functools.partial(first_kernel, n_samples, steps), grid=(2...]
  transfers between devices with their start and end apart: 3 -> 3, of which waited for: 1 -> 1; matrix products, arithmetic and copies ran while one was open for 0% -> 0% of each run, Pallas kernels for 50% -> 51%
where the time goes in v3:
time: 1270 us
  Pallas kernels  1180 us (93%)
  waiting for transfers between devices  78.1 us (6%)
  between operations  14.1 us (1%)
    pallas_call x2, Pallas kernels, block_sums(): pl.pallas_call(functools.partial(sums_kernel, 2 * layer, split), out_shap...  532 us
    pallas_call x1, Pallas kernels, first_pass(): pl.pallas_call(functools.partial(first_kernel, n_samples, steps), grid=(2...  268 us
    pallas_call x5, Pallas kernels, finish_call(): pl.pallas_call(functools.partial(finish_kernel, len(piece_specs), 1.0 / b...  216 us
    pallas_call x1, Pallas kernels, block_grad(): pl.pallas_call(functools.partial(grad_kernel, n_samples), grid=(steps,),...  99.2 us
    all_gather x2, waiting for transfers between devices, per_device(): part_a, part_b = [lax.all_gather(part, 'data') for part in pieces]  77.3 us
    pallas_call x1, Pallas kernels, add_product(): pl.pallas_call(functools.partial(add_kernel, transposed), out_shape=jax.S...  62 us
  transfers between devices with their start and end apart: 3, of which 1 were waited for; matrix products, arithmetic and copies ran while one was open for 0% of the time, Pallas kernels for 51%

profile of v3, /device:TPU:0, one launch (start us, length us, event | category | flops | bytes accessed | tf_op | source)
XLA Modules:
  0.0 1269.5 jit_solution(16391107880090381734)
XLA Ops:
  7.2 0.0 all-gather.7.cloned.1.call-start
  7.2 268.3 %first_pass.1 = (bf16[1536,8192]{1,0:T(8,128)(2,1)}, bf16[1536,8192]{1,0:T(8,128)(2,1)}, bf16[1536,8192]{1,0:T(8,128)(2,1)}, bf16[1536,8192]{1,0:T(8,128)(2,1)},...) custom-call(f32[2]{0:T(128)} %clip_ref.3, ...), custom_call_target="tpu_custom_call" | custom-call | flops 225485783040 | bytes 234881024 | tf_op jit(solution)/shard_map/first_pass/pallas_call | solution.py:142
  275.5 240.2 %sums_1.1 = bf16[32,256,256]{2,1,0:T(8,128)(2,1)} custom-call(bf16[2048,1536]{1,0:T(8,128)(2,1)} %get-tuple-element.24.xt_hbm, bf16[1536,8192]{1,0:T(8,128)(2,1)} %get-tuple-element.25.h_hbm.a_ref, bf16[1536,8192]{1,0:T(8,128)(2,1)} %get-tuple-element.26.a_hbm, bf16[2048,1536]{1,0:T(8,128)(2,1)} %get-tuple-element.27.gt_hbm, ...), custom_call_target="tpu_custom_call" | custom-call | flops 103079215104 | bytes 50331648 | tf_op jit(solution)/shard_map/sums_1/pallas_call | solution.py:453
  515.8 0.0 all-gather.7.cloned.1.call-update
  515.8 0.0 all-gather.9.cloned.1.call-start
  515.8 62.0 %add_product.1.g_ref = bf16[1536,2048]{1,0:T(8,128)(2,1)} custom-call(bf16[1536,8192]{1,0:T(8,128)(2,1)} %get-tuple-element.25.h_hbm.a_ref, bf16[2,2048,8192]{2,1,0:T(8,128)(2,1)} %w_ref.1, bf16[1536,2048]{1,0:T(8,128)(2,1)} %get-tuple-element.30.x_ref), custom_call_target="tpu_custom_call" | custom-call | flops 51539607552 | bytes 83886080 | tf_op jit(solution)/shard_map/add_product/pallas_call | solution.py:180
  577.9 99.2 %block_grad.1 = (bf16[1536,8192]{1,0:T(8,128)(2,1)}, f32[1536,1]{1,0:T(8,128)}, f32[1,1536]{1,0:T(1,128)}, bf16[2048,1536]{1,0:T(8,128)(2,1)}, bf16[2048,1536]{1,0:T(8,128)(2,1)}) custom-call(f32[2]{0:T(128)} %clip_ref.3, bf16[1536,2048]{1,0:T(8,128)(2,1)} %bitcast.55, bf16[1536,2048]{1,0:T(8,128)(2,1)} %add_product.1.g_ref, ...), custom_call_target="tpu_custom_call" | custom-call | flops 70866960384 | bytes 109051904 | tf_op jit(solution)/shard_map/block_grad/pallas_call | solution.py:221
  677.1 291.3 %sums_0.1 = (bf16[24,256,256]{2,1,0:T(8,128)(2,1)}, bf16[8,256,256]{2,1,0:T(8,128)(2,1)}) custom-call(bf16[2048,1536]{1,0:T(8,128)(2,1)} %get-tuple-element.33.xt_hbm, bf16[1536,8192]{1,0:T(8,128)(2,1)} %get-tuple-element.34.h_hbm, bf16[1536,8192]{1,0:T(8,128)(2,1)} %get-tuple-element.32.a_ref.a_hbm, bf16[2048,1536]{1,0:T(8,128)(2,1)} %get-tuple-element.35.gt_hbm, ...), custom_call_target="tpu_custom_call" | custom-call | flops 103079215104 | bytes 50331648 | tf_op jit(solution)/shard_map/sums_0/pallas_call | solution.py:453
  968.4 0.0 all-gather.9.cloned.1.call-update
  968.5 0.0 all-gather.11.cloned.1.call-start
  968.5 0.7 all-gather.11.cloned.1.call-update
  969.2 0.0 all-gather.7.cloned.1.call-done
  969.2 53.8 %finish_up_1.1.refs_17_ = f32[2,2048,8192]{2,1,0:T(8,128)} custom-call(bf16[16,32,256,256]{3,2,1,0:T(8,128)(2,1)} %bitcast.2.refs_0_.refs_1_.refs_2_.refs_3_.refs_4_.refs_5_.refs_6_.refs_7_.refs_8_.refs_9_.refs_10_.refs_11_.refs_12_.refs_13_.refs_14_.refs_15_, ...), custom_call_target="tpu_custom_call" | custom-call | flops 3355443200 | bytes 167772160 | tf_op jit(solution)/shard_map/finish_up_1/pallas_call | solution.py:489
  1023.1 53.5 %finish_down_1.1.refs_17_ = f32[2,8192,2048]{2,1,0:T(8,128)} custom-call(bf16[16,32,256,256]{3,2,1,0:T(8,128)(2,1)} %bitcast.2.refs_0_.refs_1_.refs_2_.refs_3_.refs_4_.refs_5_.refs_6_.refs_7_.refs_8_.refs_9_.refs_10_.refs_11_.refs_12_.refs_13_.refs_14_.refs_15_, ...), custom_call_target="tpu_custom_call" | custom-call | flops 3355443200 | bytes 167772160 | tf_op jit(solution)/shard_map/finish_down_1/pallas_call | solution.py:489
  1076.5 77.3 %all-gather.9.cloned.1.call-done = bf16[384,256,256]{2,1,0:T(8,128)(2,1)} async-done(((bf16[24,256,256]{2,1,0:T(8,128)(2,1)}), bf16[384,256,256]{2,1,0:T(8,128)(2,1)}) %all-gather.9.cloned.1.call-update) | async-done | bytes 50331664 | tf_op jit(solution)/shard_map/all_gather | solution.py:535
  1153.9 27.5 %finish_down_0.2.refs_17_ = f32[2,8192,2048]{2,1,0:T(8,128)} custom-call(bf16[16,24,256,256]{3,2,1,0:T(8,128)(2,1)} %bitcast.20, bf16[16,24,256,256]{3,2,1,0:T(8,128)(2,1)} %bitcast.6, bf16[16,24,256,256]{3,2,1,0:T(8,128)(2,1)} %bitcast.7, bf16[16,24,256,256]{3,2,1,0:T(8,128)(2,1)} %bitcast.8, ...), custom_call_target="tpu_custom_call", output_to_operand_aliasing={{}: (17, {})} | custom-call | flops 1677721600 | bytes 83886080 | tf_op jit(solution)/shard_map/finish_down_0/pallas_call | solution.py:489
  1181.3 53.9 %finish_up_0.1 = f32[2,2048,8192]{2,1,0:T(8,128)} custom-call(bf16[16,24,256,256]{3,2,1,0:T(8,128)(2,1)} %bitcast.21, bf16[16,24,256,256]{3,2,1,0:T(8,128)(2,1)} %bitcast.22, bf16[16,24,256,256]{3,2,1,0:T(8,128)(2,1)} %bitcast.23, bf16[16,24,256,256]{3,2,1,0:T(8,128)(2,1)} %bitcast.24, ...), custom_call_target="tpu_custom_call", output_to_operand_aliasing={{}: (17, {})} | custom-call | flops 3355443200 | bytes 167772160 | tf_op jit(solution)/shard_map/finish_up_0/pallas_call | solution.py:489
  1235.2 0.0 all-gather.11.cloned.1.call-done
  1235.2 27.5 %finish_down_0.3 = f32[2,8192,2048]{2,1,0:T(8,128)} custom-call(bf16[16,8,256,256]{3,2,1,0:T(8,128)(2,1)} %bitcast.37, bf16[16,8,256,256]{3,2,1,0:T(8,128)(2,1)} %bitcast.38, bf16[16,8,256,256]{3,2,1,0:T(8,128)(2,1)} %bitcast.39, bf16[16,8,256,256]{3,2,1,0:T(8,128)(2,1)} %bitcast.40, ...), custom_call_target="tpu_custom_call", output_to_operand_aliasing={{}: (17, {})} | custom-call | flops 1677721600 | bytes 83886080 | tf_op jit(solution)/shard_map/finish_down_0/pallas_call | solution.py:489
Async XLA Ops:
  7.2 962.0 %all-gather.7.cloned.1.call-start = ((), (), s32[]{:S(2)}) async-start(), calls=%async_computation | async-start | bytes 71303168 | tf_op jit(solution)/shard_map/all_gather | solution.py:531
  515.8 638.1 %all-gather.9.cloned.1.call-start = ((), (), s32[]{:S(2)}) async-start(), calls=%async_computation.1 | async-start | bytes 53477376 | tf_op jit(solution)/shard_map/all_gather | solution.py:535
  968.5 266.7 %all-gather.11.cloned.1.call-start = ((), (), s32[]{:S(2)}) async-start(), calls=%async_computation.2 | async-start | bytes 17825792 | tf_op jit(solution)/shard_map/all_gather | solution.py:535
Sparse Core Ops, SparseCore 0:
  515.9 297.5 all-gather.6
  968.6 185.2 all-gather.8
  1156.1 76.0 all-gather.10

commit v4 on v3

--- a/solution.py
+++ b/solution.py
@@ -13,7 +13,7 @@
 CW = 256
 PER_MAT = 16
 CHUNKS = 2 * PER_MAT
-SPLIT = 24
+BOUNDS = (4, 24, 32)
 LAG1, LAG2, LAG3 = 4, 7, 10
 RECV = 6
 OWN = 10
@@ -232,8 +232,8 @@
     return 2 * (axis + 1) + 2 * (axis // 2)
 
 
-def sums_kernel(shift, split, xt_hbm, h_hbm, a_hbm, gt_hbm, rowf, colf, r_hbm, *refs):
-    late_hbm = refs[0] if split < CHUNKS else None
+def sums_kernel(shift, bounds, xt_hbm, h_hbm, a_hbm, gt_hbm, rowf, colf, *refs):
+    outs = refs[:len(bounds)]
     (lt, slab, gpiece, clip, own, s0s, s0r, rc1, rc2, rc3, obuf,
      slab_sem, g_sem, o_sem, d_send, d_recv, sems_s, sems_r) = refs[-18:]
     me = lax.axis_index('data')
@@ -346,17 +346,16 @@
         return rows, own[chunk % OWN, rows, :].astype(F32) + recv_bufs[stage][chunk % RECV].astype(F32)
 
     def start_out(chunk):
-        @pl.when(chunk < split)
-        def _():
-            pltpu.make_async_copy(obuf.at[chunk % 2], r_hbm.at[chunk], o_sem.at[chunk % 2]).start()
-
-        if split < CHUNKS:
-            @pl.when(chunk >= split)
+        low = 0
+        for out, high in zip(outs, bounds):
+            @pl.when((chunk >= low) & (chunk < high))
             def _():
-                pltpu.make_async_copy(obuf.at[chunk % 2], late_hbm.at[chunk - split], o_sem.at[chunk % 2]).start()
+                pltpu.make_async_copy(obuf.at[chunk % 2], out.at[chunk - low], o_sem.at[chunk % 2]).start()
+
+            low = high
 
     def wait_out(chunk):
-        pltpu.make_async_copy(obuf.at[chunk % 2], r_hbm.at[0], o_sem.at[chunk % 2]).wait()
+        pltpu.make_async_copy(obuf.at[chunk % 2], outs[0].at[0], o_sem.at[chunk % 2]).wait()
 
     partner_chunk(0, True)
     g_copy(0).start()
@@ -438,7 +437,7 @@
     wait_out(CHUNKS - 1)
 
 
-def block_sums(layer, split, x_turned, h_rows, a_rows, g_turned, factors):
+def block_sums(layer, bounds, x_turned, h_rows, a_rows, g_turned, factors):
     dim, n_rows = x_turned.shape
     scratch = [
         pltpu.VMEM((2, dim, n_rows), BF16), pltpu.VMEM((4, n_rows, CW), BF16), pltpu.VMEM((CW, n_rows), BF16), pltpu.VMEM((n_rows, CW), BF16),
@@ -449,9 +448,9 @@
         pltpu.SemaphoreType.DMA((2,)), pltpu.SemaphoreType.DMA((2,)), pltpu.SemaphoreType.DMA((3, RECV)), pltpu.SemaphoreType.DMA((3, RECV)),
     ]
     flops = 4 * n_rows * dim * h_rows.shape[1]
-    sizes = (split, CHUNKS - split) if split < CHUNKS else (CHUNKS,)
+    sizes = [high - low for low, high in zip((0,) + bounds, bounds)]
     return pl.pallas_call(
-        functools.partial(sums_kernel, 2 * layer, split),
+        functools.partial(sums_kernel, 2 * layer, bounds),
         out_shape=tuple(jax.ShapeDtypeStruct((n, CW, CW), BF16) for n in sizes),
         in_specs=[ANY, ANY, ANY, ANY] + [pl.BlockSpec(memory_space=pltpu.VMEM)] * 2,
         out_specs=(ANY,) * len(sizes),
@@ -460,6 +459,74 @@
         cost_estimate=pl.CostEstimate(flops=flops, bytes_accessed=4 * n_rows * h_rows.shape[1], transcendentals=0),
         name=f'sums_{layer}',
     )(x_turned, h_rows, a_rows, g_turned, *factors)
+
+
+def deliver_kernel(shift, piece_ref, out_hbm, copy_sem, s_sem, r_sem):
+    me = lax.axis_index('data')
+    core = me % 2
+    partner = me + 1 - 2 * core
+    barrier = pltpu.get_barrier_semaphore()
+    pl.semaphore_signal(barrier, inc=1, device_id=(partner,), device_id_type=MESH_ID)
+    for axis in range(3):
+        weight = axis_weight(axis)
+        peer = me + weight * (1 - 2 * ((me // weight) % 2))
+        pl.semaphore_signal(barrier, inc=1, device_id=(peer,), device_id_type=MESH_ID)
+
+    def bit_peer(chunk, stage):
+        weight = axis_weight((chunk + shift + stage) % 3)
+        bit = (me // weight) % 2
+        return bit, me + weight * (1 - 2 * bit)
+
+    def block(chunk, stage):
+        row = sum(bit_peer(chunk, s)[0] * (1024 // 2 ** s) for s in range(3 - stage))
+        return out_hbm.at[chunk, core, pl.ds(pl.multiple_of(row, CW), CW * 2 ** stage), :]
+
+    def other_half(chunk):
+        return out_hbm.at[chunk, core, pl.ds(pl.multiple_of((1 - bit_peer(chunk, 0)[0]) * 1024, CW), 1024), :]
+
+    def placed(chunk):
+        return pltpu.make_async_copy(piece_ref.at[chunk], block(chunk, 0), copy_sem.at[chunk])
+
+    def remote(chunk, stage):
+        if stage == 0:
+            source, target, peer = piece_ref.at[chunk], block(chunk, 0), bit_peer(chunk, 2)[1]
+        elif stage < 3:
+            source, target, peer = block(chunk, stage), block(chunk, stage), bit_peer(chunk, 2 - stage)[1]
+        else:
+            part = block(chunk, 2) if stage == 3 else other_half(chunk)
+            source, target, peer = part, part, partner
+        return pltpu.make_async_remote_copy(source, target, s_sem.at[chunk, stage], r_sem.at[chunk, stage], device_id=(peer,), device_id_type=MESH_ID)
+
+    chunks = range(piece_ref.shape[0])
+    for chunk in chunks:
+        placed(chunk).start()
+    pl.semaphore_wait(barrier, 4)
+    for chunk in chunks:
+        remote(chunk, 0).start()
+    for chunk in chunks:
+        placed(chunk).wait()
+        remote(chunk, 0).wait()
+        remote(chunk, 1).start()
+    for chunk in chunks:
+        remote(chunk, 1).wait()
+        remote(chunk, 2).start()
+        remote(chunk, 3).start()
+    for chunk in chunks:
+        remote(chunk, 2).wait()
+        remote(chunk, 4).start()
+    for chunk in chunks:
+        remote(chunk, 3).wait()
+        remote(chunk, 4).wait()
+
+
+def deliver(layer, pieces):
+    n = pieces.shape[0]
+    return pl.pallas_call(
+        functools.partial(deliver_kernel, 2 * layer), out_shape=jax.ShapeDtypeStruct((n, 2, 8 * CW, CW), BF16),
+        in_specs=[pl.BlockSpec(memory_space=pltpu.VMEM)], out_specs=ANY, name='deliver',
+        scratch_shapes=[pltpu.SemaphoreType.DMA((n,)), pltpu.SemaphoreType.DMA((n, 5)), pltpu.SemaphoreType.DMA((n, 5))],
+        compiler_params=pltpu.CompilerParams(collective_id=2, has_side_effects=True),
+        cost_estimate=pl.CostEstimate(flops=40_000_000_000, bytes_accessed=n * 32 * CW * CW, transcendentals=0))(pieces)
 
 
 def owner_of(chunk, piece, half, shift):
@@ -496,14 +563,20 @@
 
 def finish_up(layer, gathered, offset, start, n, noise, prev, batch_total):
     layers, dim, ff = noise.shape
-    shift = 2 * layer
-
-    def piece_spec(c):
-        return pl.BlockSpec((1, 1, CW, CW), lambda i, k, c=c: (owner_of(start + c, i, k, shift), start - offset + c, 0, 0))
-
-    per_half = ff // 2 // (n * CW)
-    tile = pl.BlockSpec((1, CW, n * CW), lambda i, k: (layer, i, k * per_half + start // n))
-    return finish_call('finish_up', layer, (dim // CW, 2), [piece_spec(c) for c in range(n)], tile, gathered, noise, prev, batch_total)
+    shift, across = 2 * layer, 2
+
+    def piece_spec(piece, c):
+        def index(k, group):
+            chunk = start + across * group + c
+            if offset is None:
+                return chunk, k, piece, 0
+            return owner_of(chunk, piece, k, shift), chunk - offset, 0, 0
+
+        return pl.BlockSpec((1, 1, CW, CW), index)
+
+    tile = pl.BlockSpec((1, dim, across * CW), lambda k, group: (layer, 0, (k * PER_MAT + start) // across + group))
+    specs = [piece_spec(piece, c) for piece in range(dim // CW) for c in range(across)]
+    return finish_call('finish_up', layer, (2, n // across), specs, tile, gathered, noise, prev, batch_total)
 
 
 def finish_down(layer, gathered, offset, start, n, noise, prev, batch_total):
@@ -527,19 +600,23 @@
     n_rows = n_samples * seq_len
     x_first = x_in.reshape(n_rows, dim)
     z_first, a_first, a_last, h_last, row_f, col_f, x_turned, g_turned, g_last = first_pass(x_first, dy_out.reshape(n_rows, dim), w_up, w_down, clip_norm, lengths)
-    piece, = block_sums(1, CHUNKS, x_turned, h_last, a_last, g_turned, (row_f, col_f))
+    piece, = block_sums(1, (CHUNKS,), x_turned, h_last, a_last, g_turned, (row_f, col_f))
     gathered_last = lax.all_gather(piece, 'data')
     g_first = add_product(1, g_last, h_last, w_up, True)
     h_first, row_f, col_f, x_turned, g_turned = block_grad(x_first, g_first, z_first, a_first, w_down, clip_norm, n_samples)
-    pieces = block_sums(0, SPLIT, x_turned, h_first, a_first, g_turned, (row_f, col_f))
-    part_a, part_b = [lax.all_gather(part, 'data') for part in pieces]
+    early, piece_a, piece_b = block_sums(0, BOUNDS, x_turned, h_first, a_first, g_turned, (row_f, col_f))
+    first, second, _ = BOUNDS
+    part_a, part_b = [lax.all_gather(part, 'data') for part in (piece_a, piece_b)]
+    early = deliver(0, early)
+    gathered_last, early = lax.optimization_barrier((gathered_last, early))
     grad_up = finish_up(1, gathered_last, 0, 0, PER_MAT, noise_up, None, batch_total)
     grad_down = finish_down(1, gathered_last, 0, PER_MAT, PER_MAT, noise_down, None, batch_total)
+    grad_up = finish_up(0, early, None, 0, first, noise_up, grad_up, batch_total)
     grad_up, grad_down, part_a = lax.optimization_barrier((grad_up, grad_down, part_a))
-    grad_up = finish_up(0, part_a, 0, 0, PER_MAT, noise_up, grad_up, batch_total)
-    grad_down = finish_down(0, part_a, 0, PER_MAT, SPLIT - PER_MAT, noise_down, grad_down, batch_total)
+    grad_up = finish_up(0, part_a, first, first, PER_MAT - first, noise_up, grad_up, batch_total)
+    grad_down = finish_down(0, part_a, first, PER_MAT, second - PER_MAT, noise_down, grad_down, batch_total)
     grad_up, grad_down, part_b = lax.optimization_barrier((grad_up, grad_down, part_b))
-    grad_down = finish_down(0, part_b, SPLIT, SPLIT, CHUNKS - SPLIT, noise_down, grad_down, batch_total)
+    grad_down = finish_down(0, part_b, second, second, CHUNKS - second, noise_down, grad_down, batch_total)
     return grad_up, grad_down
 
 

time: 1270 us -> 1270 us (level)
  waiting for transfers between devices: 78.1 us -> 2.62 us
  Pallas kernels: 1180 us -> 1240 us
    all_gather x2, waiting for transfers between devices: 77.3 us -> 1.89 us  [per_device(): lax.all_gather(part, 'data')]
    pallas_call x2 -> x3, Pallas kernels: 532 us -> 592 us  [the longest x2 532 us: block_sums(): pl.pallas_call(functools.partial(sums_kernel, 2 * layer, bounds), out_sha...]
    pallas_call x5 -> x6, Pallas kernels: 216 us -> 220 us  [finish_call(): pl.pallas_call(functools.partial(finish_kernel, len(piece_specs), 1.0 / b...]
  transfers between devices with their start and end apart: 3 -> 3, of which waited for: 1 -> 1; matrix products, arithmetic and copies ran while one was open for 0% -> 0% of each run, Pallas kernels for 51% -> 56%
where the time goes in v4:
time: 1270 us; the launch traced here: 1260 us
  Pallas kernels  1240 us (98%)
  between operations  14.2 us (1%)
    pallas_call x2, Pallas kernels, block_sums(): pl.pallas_call(functools.partial(sums_kernel, 2 * layer, bounds), out_sha...  532 us
    pallas_call x1, Pallas kernels, first_pass(): pl.pallas_call(functools.partial(first_kernel, n_samples, steps), grid=(2...  268 us
    pallas_call x6, Pallas kernels, finish_call(): pl.pallas_call(functools.partial(finish_kernel, len(piece_specs), 1.0 / b...  220 us
    pallas_call x1, Pallas kernels, block_grad(): pl.pallas_call(functools.partial(grad_kernel, n_samples), grid=(steps,),...  99.3 us
    pallas_call x1, Pallas kernels, add_product(): pl.pallas_call(functools.partial(add_kernel, transposed), out_shape=jax.S...  62 us
    pallas_call x1, Pallas kernels, deliver(): pl.pallas_call(functools.partial(deliver_kernel, 2 * layer), out_shape=ja...  60.5 us
  transfers between devices with their start and end apart: 3, of which 1 were waited for; matrix products, arithmetic and copies ran while one was open for 0% of the time, Pallas kernels for 56%

profile of v4, /device:TPU:0, one launch (start us, length us, event | category | flops | bytes accessed | tf_op | source)
XLA Modules:
  0.0 1258.8 jit_solution(5671095899395131007)
XLA Ops:
  7.2 0.0 all-gather.7.cloned.1.call-start
  7.2 268.3 %first_pass.1 = (bf16[1536,8192]{1,0:T(8,128)(2,1)}, bf16[1536,8192]{1,0:T(8,128)(2,1)}, bf16[1536,8192]{1,0:T(8,128)(2,1)}, bf16[1536,8192]{1,0:T(8,128)(2,1)},...) custom-call(f32[2]{0:T(128)} %clip_ref.3, ...), custom_call_target="tpu_custom_call" | custom-call | flops 225485783040 | bytes 234881024 | tf_op jit(solution)/shard_map/first_pass/pallas_call | solution.py:142
  275.5 240.2 %sums_1.1 = bf16[32,256,256]{2,1,0:T(8,128)(2,1)} custom-call(bf16[2048,1536]{1,0:T(8,128)(2,1)} %get-tuple-element.27.xt_hbm, bf16[1536,8192]{1,0:T(8,128)(2,1)} %get-tuple-element.28.h_hbm.a_ref, bf16[1536,8192]{1,0:T(8,128)(2,1)} %get-tuple-element.29.a_hbm, bf16[2048,1536]{1,0:T(8,128)(2,1)} %get-tuple-element.30.gt_hbm, ...), custom_call_target="tpu_custom_call" | custom-call | flops 103079215104 | bytes 50331648 | tf_op jit(solution)/shard_map/sums_1/pallas_call | solution.py:452
  515.8 0.0 all-gather.7.cloned.1.call-update
  515.8 0.0 all-gather.9.cloned.1.call-start
  515.8 62.0 %add_product.1.g_ref = bf16[1536,2048]{1,0:T(8,128)(2,1)} custom-call(bf16[1536,8192]{1,0:T(8,128)(2,1)} %get-tuple-element.28.h_hbm.a_ref, bf16[2,2048,8192]{2,1,0:T(8,128)(2,1)} %w_ref.1, bf16[1536,2048]{1,0:T(8,128)(2,1)} %get-tuple-element.33.x_ref), custom_call_target="tpu_custom_call" | custom-call | flops 51539607552 | bytes 83886080 | tf_op jit(solution)/shard_map/add_product/pallas_call | solution.py:180
  577.8 99.3 %block_grad.1 = (bf16[1536,8192]{1,0:T(8,128)(2,1)}, f32[1536,1]{1,0:T(8,128)}, f32[1,1536]{1,0:T(1,128)}, bf16[2048,1536]{1,0:T(8,128)(2,1)}, bf16[2048,1536]{1,0:T(8,128)(2,1)}) custom-call(f32[2]{0:T(128)} %clip_ref.3, bf16[1536,2048]{1,0:T(8,128)(2,1)} %bitcast.55, bf16[1536,2048]{1,0:T(8,128)(2,1)} %add_product.1.g_ref, ...), custom_call_target="tpu_custom_call" | custom-call | flops 70866960384 | bytes 109051904 | tf_op jit(solution)/shard_map/block_grad/pallas_call | solution.py:221
  677.1 291.3 %sums_0.1 = (bf16[4,256,256]{2,1,0:T(8,128)(2,1)}, bf16[20,256,256]{2,1,0:T(8,128)(2,1)}, bf16[8,256,256]{2,1,0:T(8,128)(2,1)}) custom-call(bf16[2048,1536]{1,0:T(8,128)(2,1)} %get-tuple-element.36.xt_hbm, bf16[1536,8192]{1,0:T(8,128)(2,1)} %get-tuple-element.37.h_hbm, bf16[1536,8192]{1,0:T(8,128)(2,1)} %get-tuple-element.35.a_ref.a_hbm, ...), custom_call_target="tpu_custom_call" | custom-call | flops 103079215104 | bytes 50331648 | tf_op jit(solution)/shard_map/sums_0/pallas_call | solution.py:452
  968.4 0.0 all-gather.9.cloned.1.call-update
  968.5 0.0 all-gather.11.cloned.1.call-start
  968.5 0.7 all-gather.11.cloned.1.call-update
  969.2 60.5 %deliver.1.refs_0_.refs_1_.refs_2_.refs_3_.refs_4_.refs_5_.refs_6_.refs_7_.refs_8_.refs_9_.refs_10_.refs_11_.refs_12_.refs_13_.refs_14_.refs_15_ = bf16[4,2,2048,256]{3,2,1,0:T(8,128)(2,1)} custom-call(bf16[4,256,256]{2,1,0:T(8,128)(2,1)} %get-tuple-element.41.piece_ref), custom_call_target="tpu_custom_call" | custom-call | flops 40000000000 | bytes 8388608 | tf_op jit(solution)/shard_map/deliver/pallas_call | solution.py:524
  1029.8 0.0 all-gather.7.cloned.1.call-done
  1029.8 55.0 %finish_up_1.1.refs_17_ = f32[2,2048,8192]{2,1,0:T(8,128)} custom-call(bf16[16,32,256,256]{3,2,1,0:T(8,128)(2,1)} %bitcast.2.refs_0_.refs_1_.refs_2_.refs_3_.refs_4_.refs_5_.refs_6_.refs_7_.refs_8_.refs_9_.refs_10_.refs_11_.refs_12_.refs_13_.refs_14_.refs_15_, ...), custom_call_target="tpu_custom_call" | custom-call | flops 3355443200 | bytes 167772160 | tf_op jit(solution)/shard_map/finish_up_1/pallas_call | solution.py:556
  1084.8 15.0 %finish_up_0.2.refs_17_ = f32[2,2048,8192]{2,1,0:T(8,128)} custom-call(bf16[4,2,2048,256]{3,2,1,0:T(8,128)(2,1)} %deliver.1.refs_0_.refs_1_.refs_2_.refs_3_.refs_4_.refs_5_.refs_6_.refs_7_.refs_8_.refs_9_.refs_10_.refs_11_.refs_12_.refs_13_.refs_14_.refs_15_, ...), custom_call_target="tpu_custom_call", output_to_operand_aliasing={{}: (17, {})} | custom-call | flops 838860800 | bytes 41943040 | tf_op jit(solution)/shard_map/finish_up_0/pallas_call | solution.py:556
  1099.8 53.5 %finish_down_1.1.refs_17_ = f32[2,8192,2048]{2,1,0:T(8,128)} custom-call(bf16[16,32,256,256]{3,2,1,0:T(8,128)(2,1)} %bitcast.2.refs_0_.refs_1_.refs_2_.refs_3_.refs_4_.refs_5_.refs_6_.refs_7_.refs_8_.refs_9_.refs_10_.refs_11_.refs_12_.refs_13_.refs_14_.refs_15_, ...), custom_call_target="tpu_custom_call" | custom-call | flops 3355443200 | bytes 167772160 | tf_op jit(solution)/shard_map/finish_down_1/pallas_call | solution.py:556
  1153.3 0.0 all-gather.9.cloned.1.call-done
  1153.3 27.5 %finish_down_0.2.refs_17_ = f32[2,8192,2048]{2,1,0:T(8,128)} custom-call(bf16[16,20,256,256]{3,2,1,0:T(8,128)(2,1)} %bitcast.20, bf16[16,20,256,256]{3,2,1,0:T(8,128)(2,1)} %bitcast.6, bf16[16,20,256,256]{3,2,1,0:T(8,128)(2,1)} %bitcast.7, bf16[16,20,256,256]{3,2,1,0:T(8,128)(2,1)} %bitcast.8, ...), custom_call_target="tpu_custom_call", output_to_operand_aliasing={{}: (17, {})} | custom-call | flops 1677721600 | bytes 83886080 | tf_op jit(solution)/shard_map/finish_down_0/pallas_call | solution.py:556
  1180.8 41.7 %finish_up_0.3 = f32[2,2048,8192]{2,1,0:T(8,128)} custom-call(bf16[16,20,256,256]{3,2,1,0:T(8,128)(2,1)} %bitcast.21, bf16[16,20,256,256]{3,2,1,0:T(8,128)(2,1)} %bitcast.22, bf16[16,20,256,256]{3,2,1,0:T(8,128)(2,1)} %bitcast.23, bf16[16,20,256,256]{3,2,1,0:T(8,128)(2,1)} %bitcast.24, ...), custom_call_target="tpu_custom_call", output_to_operand_aliasing={{}: (17, {})} | custom-call | flops 2516582400 | bytes 125829120 | tf_op jit(solution)/shard_map/finish_up_0/pallas_call | solution.py:556
  1222.6 1.9 all-gather.11.cloned.1.call-done
  1224.4 27.5 %finish_down_0.3 = f32[2,8192,2048]{2,1,0:T(8,128)} custom-call(bf16[16,8,256,256]{3,2,1,0:T(8,128)(2,1)} %bitcast.37, bf16[16,8,256,256]{3,2,1,0:T(8,128)(2,1)} %bitcast.38, bf16[16,8,256,256]{3,2,1,0:T(8,128)(2,1)} %bitcast.39, bf16[16,8,256,256]{3,2,1,0:T(8,128)(2,1)} %bitcast.40, ...), custom_call_target="tpu_custom_call", output_to_operand_aliasing={{}: (17, {})} | custom-call | flops 1677721600 | bytes 83886080 | tf_op jit(solution)/shard_map/finish_down_0/pallas_call | solution.py:556
Async XLA Ops:
  7.2 1022.6 %all-gather.7.cloned.1.call-start = ((), (), s32[]{:S(2)}) async-start(), calls=%async_computation | async-start | bytes 71303168 | tf_op jit(solution)/shard_map/all_gather | solution.py:604
  515.8 637.5 %all-gather.9.cloned.1.call-start = ((), (), s32[]{:S(2)}) async-start(), calls=%async_computation.1 | async-start | bytes 44564480 | tf_op jit(solution)/shard_map/all_gather | solution.py:609
  968.5 255.9 %all-gather.11.cloned.1.call-start = ((), (), s32[]{:S(2)}) async-start(), calls=%async_computation.2 | async-start | bytes 17825792 | tf_op jit(solution)/shard_map/all_gather | solution.py:609
Sparse Core Ops, SparseCore 0:
  515.9 297.5 all-gather.6
  968.6 177.4 all-gather.8
  1148.3 76.0 all-gather.10
